TPU v7x, 128 devices: a whole 4x4x4 slice. The times are simulated.
128 devices in a mesh: vert: 32 (over x, y, core), feat: 4 (over z).
Axes of the slice: x: 4, y: 4, z: 4, core: 2. Of those that a mesh axis runs over, the one named last changes fastest.
Arguments:
- features: bfloat16 [256, 262144], P('feat', 'vert'), may hold values from -6 to 6
- tile_vals: bfloat16 [16384, 128, 128], P('vert'), may hold values from -0.1875 to 0.1875
- tile_row: int32 [32, 512], P('vert'), may hold values from 0 to 63
- tile_col: int32 [32, 512], P('vert'), may hold values from 0 to 95
- tile_count: int32 [32], P('vert'), may hold values from 1 to 512, as said below
- recv_rows: int32 [32, 32, 128], P('vert'), may hold values from 0 to 8191
- recv_count: int32 [32, 32], P('vert'), may hold values from 0 to 128, as said below
- weight: bfloat16 [256, 256], replicated, may hold values from -0.375 to 0.375
- bias: float32 [256], replicated, may hold values from -4 to 4
Outputs:
- layer_out: bfloat16 [262144, 256], P(('vert', 'feat'))
Inputs may be any that keep to these rules, and one draw needn't show every extreme that they name: `tile_count`: tile slots at or past a partition's count are padding with arbitrary contents; some partition uses all 512 slots. `recv_count`: slots at or past the count hold arbitrary valid vertices; some pair uses all 128 slots.
All inputs are finite; a program needn't handle non-finite values.
Results may differ from a plain program's by a relative error of at most 0.0075.
Values may be sent and summed in bfloat16 or wider, within the bound.
No kernel may reach another device: no remote copies, remote signals or barrier semaphores. Data moves between devices by JAX's collectives and lax.ppermute only.
A program may use at most 256 MiB of HBM per device.

v0:
```python
import jax
import jax.numpy as jnp
from jax import lax
from jax.sharding import PartitionSpec as P


def on_device(
    features, tile_vals, tile_row, tile_col, tile_count, recv_rows, recv_count, weight, bias
):
    parts = lax.axis_size("vert")
    width = features.shape[0]
    v_rows = features.shape[1]
    slots = recv_rows.shape[2]
    asked = recv_rows[0]
    wanted = lax.all_to_all(asked, "vert", split_axis=0, concat_axis=0, tiled=True)
    outgoing = features[:, wanted.reshape(-1)].reshape(width, parts, slots)
    remote = lax.all_to_all(outgoing, "vert", split_axis=1, concat_axis=1, tiled=True)
    usable = jnp.arange(slots, dtype=jnp.int32)[None, :] < recv_count[0][:, None]
    remote = jnp.where(usable[None, :, :], remote, jnp.zeros_like(remote))
    rowbuf = jnp.concatenate([features, remote.reshape(width, parts * slots)], axis=1)
    tile_size = tile_vals.shape[1]
    blocks = rowbuf.reshape(width, -1, tile_size)[:, tile_col[0]]
    product = jnp.einsum("ftj,tij->tfi", blocks, tile_vals, preferred_element_type=jnp.float32)
    n_tiles = tile_vals.shape[0]
    used = jnp.arange(n_tiles, dtype=jnp.int32) < tile_count[0]
    row_blocks = v_rows // tile_size
    onehot = (
        (tile_row[0][None, :] == jnp.arange(row_blocks, dtype=jnp.int32)[:, None]) & used[None, :]
    ).astype(jnp.bfloat16)
    upper = product.astype(jnp.bfloat16)
    lower = (product - upper.astype(jnp.float32)).astype(jnp.bfloat16)
    aggregate = jnp.einsum("rt,tfi->fri", onehot, upper, preferred_element_type=jnp.float32)
    aggregate = aggregate + jnp.einsum(
        "rt,tfi->fri", onehot, lower, preferred_element_type=jnp.float32
    )
    aggregate = aggregate.reshape(width, v_rows).astype(jnp.bfloat16)
    gathered = lax.all_to_all(aggregate, "feat", split_axis=1, concat_axis=0, tiled=True)
    hidden = (
        lax.dot_general(
            gathered, weight, (((0,), (0,)), ((), ())), preferred_element_type=jnp.float32
        )
        + bias
    )
    return jnp.maximum(hidden, 0.0).astype(jnp.bfloat16)


def solution(mesh):
    in_specs = (
        P("feat", "vert"),
        P("vert", None, None),
        P("vert", None),
        P("vert", None),
        P("vert"),
        P("vert", None, None),
        P("vert", None),
        P(),
        P(),
    )
    out_specs = P(("vert", "feat"), None)
    return jax.shard_map(
        on_device, mesh=mesh, in_specs=in_specs, out_specs=out_specs, check_vma=False
    )
```

profile of v0, /device:TPU:1, one launch (start us, length us, event | category | flops | bytes accessed | tf_op | source)
XLA Modules:
  0.0 115.7 jit_solution(13095355253474465088)
XLA Ops:
  0.0 0.0 copy-start
  0.0 0.0 copy-start.1
  0.0 0.0 copy-start.2
  0.0 0.0 copy-start.3
  0.0 8.7 %all-to-all-start = ((s32[32,1,128]{2,1,0:T(1,128)}), s32[32,1,128]{2,1,0:T(1,128)S(1)}, u32[]{:S(2)}, u32[]{:S(2)}) async-start(s32[32,1,128]{2,1,0:T(1,128)} %bitcast.44), calls=%async_computation | async-start | bytes 32768 | tf_op jit(solution)/shard_map/all_to_all | solution.py:15
  9.4 2.0 %copy.31 = bf16[64,8192]{0,1:T(8,128)(2,1)S(1)} copy(bf16[64,8192]{1,0:T(8,128)(2,1)} %param.9) | data formatting | bytes 2097152 | tf_op args[0]
  11.4 4.2 %all-to-all-done = s32[32,1,128]{2,1,0:T(1,128)S(1)} async-done(((s32[32,1,128]{2,1,0:T(1,128)}), s32[32,1,128]{2,1,0:T(1,128)S(1)}, u32[]{:S(2)}, u32[]{:S(2)}) %all-to-all-start) | async-done | bytes 16416 | tf_op jit(solution)/shard_map/all_to_all | solution.py:15
  15.7 15.0 %gather_fusion = bf16[4096,64]{1,0:T(8,128)(2,1)} fusion(bf16[64,8192]{0,1:T(8,128)(2,1)S(1)} %copy.31, s32[4096]{0:T(1024)S(1)} %broadcast_clamp_fusion), kind=kCustom, calls=%fused_computation | custom fusion | bytes 1064960 | tf_op jit(solution)/shard_map/gather | solution.py:16
  30.7 2.3 %copy.32 = bf16[64,32,128]{2,0,1:T(8,128)(2,1)} copy(bf16[64,32,128]{0,2,1:T(8,128)(2,1)} %bitcast.41) | data formatting | bytes 1048576 | tf_op jit(solution)/shard_map/reshape | solution.py:16
  33.1 4.2 %all-to-all-start.1 = ((bf16[64,32,128]{2,0,1:T(8,128)(2,1)}), bf16[64,32,128]{2,0,1:T(8,128)(2,1)S(1)}, u32[]{:S(2)}, u32[]{:S(2)}) async-start(bf16[64,32,128]{2,0,1:T(8,128)(2,1)} %copy.32), calls=%async_computation.1 | async-start | bytes 1048576 | tf_op jit(solution)/shard_map/all_to_all | solution.py:17
  37.3 0.0 copy-done.2
  37.3 0.0 copy-done.3
  37.3 0.1 iota_compare_fusion.1
  37.4 11.6 %all-to-all-done.1 = bf16[64,32,128]{2,0,1:T(8,128)(2,1)S(1)} async-done(((bf16[64,32,128]{2,0,1:T(8,128)(2,1)}), bf16[64,32,128]{2,0,1:T(8,128)(2,1)S(1)}, u32[]{:S(2)}, u32[]{:S(2)}) %all-to-all-start.1) | async-done | bytes 524320 | tf_op jit(solution)/shard_map/all_to_all | solution.py:17
  49.0 0.1 copy_bitcast_fusion.1
  49.1 0.0 copy-done.1
  49.1 0.4 copy_bitcast_fusion
  49.5 13.5 %gather_fusion.1 = bf16[512,64,128]{2,1,0:T(8,128)(2,1)} fusion(bf16[64,96,128]{2,0,1:T(8,128)(2,1)S(1)} %copy_bitcast_fusion, s32[1024]{0:T(1024)S(1)} %pad_clamp_fusion), kind=kCustom, calls=%fused_computation.1 | custom fusion | bytes 16779264 | tf_op jit(solution)/shard_map/gather | solution.py:22
  63.0 0.0 copy-start.4
  63.0 17.3 %subtract_convert_fusion = (bf16[512,64,128]{2,1,0:T(8,128)(2,1)}, bf16[512,64,128]{2,1,0:T(8,128)(2,1)S(1)}) fusion(bf16[512,128,128]{2,1,0:T(8,128)(2,1)} %param.10, bf16[512,64,128]{2,1,0:T(8,128)(2,1)} %gather_fusion.1), kind=kOutput, calls=%fused_computation.2 | convolution fusion | flops 1090519040 | bytes 41943040 | tf_op jit(solution)/shard_map/ftj,tij->tfi/dot_general | solution.py:23
  80.3 0.0 copy-done.4
  80.3 8.3 %fusion.2 = f32[64,128,64]{1,2,0:T(8,128)S(1)} fusion(bf16[512,64,128]{2,1,0:T(8,128)(2,1)} %get-tuple-element.5, s32[512]{0:T(512)S(1)} %bitcast.47, pred[512]{0:T(512)(128)(4,1)S(1)} %iota_compare_fusion.2), kind=kOutput, calls=%fused_computation.5 | convolution fusion | flops 536936448 | bytes 10488320 | tf_op jit(solution)/shard_map/rt,tfi->fri/dot_general | solution.py:33
  88.6 0.0 copy-start.5
  88.6 5.0 %fusion.10 = bf16[64,64,128]{2,1,0:T(8,128)(2,1)S(1)} fusion(f32[64,128,64]{1,2,0:T(8,128)S(1)} %fusion.2, bf16[512,64,128]{2,1,0:T(8,128)(2,1)S(1)} %get-tuple-element.6, s32[512]{0:T(512)S(1)} %bitcast.48, pred[512]{0:T(512)(128)(4,1)S(1)} %iota_compare_fusion.2), kind=kOutput, calls=%fused_computation.15 | convolution fusion | flops 537985024 | bytes 11536896 | tf_op jit(solution)/shard_map/rt,tfi->fri/dot_general | solution.py:32
  93.6 0.3 convert_element_type.28
  93.9 0.6 copy.37
  94.5 19.7 %all_to_all.30 = bf16[64,4,2048]{2,0,1:T(8,128)(2,1)S(1)} all-to-all(bf16[64,4,2048]{2,0,1:T(8,128)(2,1)S(1)} %copy.37), channel_id=1, replica_groups=mesh['vert'=32,'feat'=4] {'feat'}, dimensions={1} | all-to-all | bytes 2097152 | tf_op jit(solution)/shard_map/all_to_all | solution.py:37
  114.2 0.0 copy-done
  114.2 0.0 copy-done.5
  114.2 1.5 %fusion.7 = bf16[2048,256]{1,0:T(8,128)(2,1)} fusion(bf16[256,2048]{1,0:T(8,128)(2,1)S(1)} %bitcast.42, bf16[256,256]{1,0:T(8,128)(2,1)S(1)} %copy-done, f32[256]{0:T(256)S(1)} %copy-done.5), kind=kOutput, calls=%fused_computation.11 | convolution fusion | flops 270008320 | bytes 2229248 | tf_op jit(solution)/shard_map/dot_general | solution.py:39
  (5 shorter events, 0.0 us)
Async XLA Ops:
  0.0 114.2 %copy-start = (bf16[256,256]{1,0:T(8,128)(2,1)S(1)}, bf16[256,256]{1,0:T(8,128)(2,1)}, u32[]{:S(2)}) copy-start(bf16[256,256]{1,0:T(8,128)(2,1)} %param.16) | copy-start | bytes 393220
  0.0 49.1 %copy-start.1 = (bf16[64,8192]{1,0:T(8,128)(2,1)S(1)}, bf16[64,8192]{1,0:T(8,128)(2,1)}, u32[]{:S(2)}) copy-start(bf16[64,8192]{1,0:T(8,128)(2,1)} %param.9) | copy-start | bytes 3145732
  0.0 37.3 %copy-start.2 = (s32[1,512]{1,0:T(1,128)S(1)}, s32[1,512]{1,0:T(1,128)}, u32[]{:S(2)}) copy-start(s32[1,512]{1,0:T(1,128)} %param.12) | copy-start | bytes 6148
  0.0 37.3 %copy-start.3 = (s32[1,32]{1,0:T(1,128)S(1)}, s32[1,32]{1,0:T(1,128)}, u32[]{:S(2)}) copy-start(s32[1,32]{1,0:T(1,128)} %param.15) | copy-start | bytes 388
  0.0 15.6 %all-to-all-start = ((s32[32,1,128]{2,1,0:T(1,128)}), s32[32,1,128]{2,1,0:T(1,128)S(1)}, u32[]{:S(2)}, u32[]{:S(2)}) async-start(s32[32,1,128]{2,1,0:T(1,128)} %bitcast.44), calls=%async_computation | async-start | bytes 32768 | tf_op jit(solution)/shard_map/all_to_all | solution.py:15
  33.1 15.9 %all-to-all-start.1 = ((bf16[64,32,128]{2,0,1:T(8,128)(2,1)}), bf16[64,32,128]{2,0,1:T(8,128)(2,1)S(1)}, u32[]{:S(2)}, u32[]{:S(2)}) async-start(bf16[64,32,128]{2,0,1:T(8,128)(2,1)} %copy.32), calls=%async_computation.1 | async-start | bytes 1048576 | tf_op jit(solution)/shard_map/all_to_all | solution.py:17
  63.0 17.3 %copy-start.4 = (s32[1,512]{1,0:T(1,128)S(1)}, s32[1,512]{1,0:T(1,128)}, u32[]{:S(2)}) copy-start(s32[1,512]{1,0:T(1,128)} %param.11) | copy-start | bytes 6148
  88.6 25.6 %copy-start.5 = (f32[256]{0:T(256)S(1)}, f32[256]{0:T(256)}, u32[]{:S(2)}) copy-start(f32[256]{0:T(256)} %param.17) | copy-start | bytes 3076
where the time goes:
time: 116 us
  local copies, waits for them, and re-layouts  33.8 us (29%)
  matrix products  32.1 us (28%)
  blocking collectives  19.7 us (17%)
  waiting for transfers between devices  15.8 us (14%)
  starting transfers between devices  12.9 us (11%)
    all_to_all x1, blocking collectives, on_device(): lax.all_to_all(aggregate, 'feat', split_axis=1, concat_axis=0, tiled=True)  19.7 us
    dot_general x1, matrix products, on_device(): jnp.einsum('ftj,tij->tfi', blocks, tile_vals, preferred_element_type=jnp....  17.3 us
    gather x1, local copies, waits for them, and re-layouts, on_device(): outgoing = features[:, wanted.reshape(-1)].reshape(width, parts, slots)  15 us
    gather x1, local copies, waits for them, and re-layouts, on_device(): blocks = rowbuf.reshape(width, -1, tile_size)[:, tile_col[0]]  13.5 us
    all_to_all x1, waiting for transfers between devices, on_device(): lax.all_to_all(outgoing, 'vert', split_axis=1, concat_axis=1, tiled=True)  11.6 us
    all_to_all x1, starting transfers between devices, on_device(): lax.all_to_all(asked, 'vert', split_axis=0, concat_axis=0, tiled=True)  8.72 us
    dot_general x1, matrix products, on_device(): jnp.einsum('rt,tfi->fri', onehot, lower, preferred_element_type=jnp.float32)  8.26 us
    dot_general x1, matrix products, on_device(): jnp.einsum('rt,tfi->fri', onehot, upper, preferred_element_type=jnp.float32)  5.02 us
  transfers between devices with their start and end apart: 2, of which 2 were waited for; matrix products, arithmetic and copies ran while one was open for 2% of the time, Pallas kernels for 0%

commit v1 on v0

v1 whole, which is shorter than its diff:
```python
import jax
import jax.numpy as jnp
from jax import lax
from jax.experimental import pallas as pl
from jax.experimental.pallas import tpu as pltpu
from jax.sharding import PartitionSpec as P

U = 8
DEPTH = 5
NT = (((1,), (1,)), ((), ()))
TN = (((0,), (0,)), ((), ()))
VMEM = pl.BlockSpec(memory_space=pltpu.VMEM)
HBM = pl.BlockSpec(memory_space=pltpu.HBM)
SMEM = pl.BlockSpec(memory_space=pltpu.SMEM)
BF, F32, I32 = jnp.bfloat16, jnp.float32, jnp.int32


def params(mib):
    return pltpu.CompilerParams(vmem_limit_bytes=mib << 20)


def cost(flops, nbytes):
    return pl.CostEstimate(flops=flops, bytes_accessed=nbytes, transcendentals=0)


def tile_lists(tile_row, tile_col, tile_count):
    n = tile_row.shape[0]
    t = jnp.arange(n, dtype=I32)
    far = (tile_col >= 64).astype(I32)
    key = jnp.where(t < tile_count, tile_row + 64 * far, 128)
    b = jnp.arange(128, dtype=I32)
    member = (key[None, :] == b[:, None]).astype(I32)
    pairs = (jnp.sum(member, axis=1) + 1) // 2
    before = jnp.sum(jnp.where(b[None, :] < b[:, None], pairs[None, :], 0), axis=1)
    local = jnp.sum(jnp.where(b < 64, pairs, 0))
    first = (local + U - 1) // U * U
    end = first + jnp.sum(jnp.where(b < 64, 0, pairs))
    base = before + jnp.where(b < 64, 0, first - local)
    place = jnp.sum(
        ((key[None, :] == key[:, None]) & (t[None, :] < t[:, None])).astype(I32), axis=1
    )
    slot = 2 * jnp.sum(member * base[:, None], axis=0) + place
    slot = jnp.where(key < 128, slot, -1)
    entry = t | (tile_row << 9) | ((tile_col - 64 * far + 1) << 15)
    s = jnp.arange(640 + 4 * U, dtype=I32)
    entries = jnp.sum(jnp.where(slot[None, :] == s[:, None], entry[None, :], 0), axis=1)
    return entries, jnp.stack([first, end])


def table_kernel(x_ref, out_ref):
    half = out_ref.shape[0]

    def step(k, _):
        at = pl.multiple_of(k * 128, 128)
        x = jnp.concatenate([x_ref[:, pl.ds(at, 128)], x_ref[:, pl.ds(at + half, 128)]], axis=0)
        out_ref[pl.ds(at, 128), :] = x.astype(F32).T
        return 0

    lax.fori_loop(0, half // 128, step, 0, unroll=4)


def gather_kernel(idx_ref, which_ref, table_ref, out_ref, rows_ref, buf, sem):
    half = table_ref.shape[0]

    def step(p, _):
        for s in range(128):
            rows_ref[s : s + 1, :] = table_ref[idx_ref[p, s] & (half - 1)]
        g = rows_ref[...].T
        buf[p] = jnp.where(which_ref[p] < half, g[:64], g[64:]).astype(BF)
        pltpu.make_async_copy(buf.at[p], out_ref.at[p], sem).start()
        return 0

    lax.fori_loop(0, out_ref.shape[0], step, 0)
    pltpu.make_async_copy(buf, out_ref, sem).wait()


class Tiles:
    def __init__(self, start, end, list_ref, vals_ref, buf, sems):
        self.start, self.list, self.vals, self.buf, self.sems = start, list_ref, vals_ref, buf, sems
        self.groups = (end - start + U - 1) // U

    def fetch(self, c):
        slot = lax.rem(c, DEPTH)
        for k in range(2 * U):
            e = self.list[2 * (self.start + c * U) + k]
            pltpu.make_async_copy(
                self.vals.at[e & 511], self.buf.at[slot * 2 * U + k], self.sems.at[slot]
            ).start()

    def begin(self):
        def step(c, _):
            self.fetch(c)
            return 0

        lax.fori_loop(0, jnp.minimum(self.groups, DEPTH - 1), step, 0)

    def add(self, block, acc_ref):
        def step(c, _):
            @pl.when(c + DEPTH - 1 < self.groups)
            def _():
                self.fetch(c + DEPTH - 1)

            slot = lax.rem(c, DEPTH)
            here = pl.ds(pl.multiple_of(slot * 2 * U, 2 * U), 2 * U)
            pltpu.make_async_copy(
                self.vals.at[pl.ds(0, 2 * U)], self.buf.at[here], self.sems.at[slot]
            ).wait()
            found = []
            for u in range(U):
                at = 2 * (self.start + c * U + u)
                e, f = self.list[at], self.list[at + 1]
                at = slot * 2 * U + 2 * u
                lhs = jnp.concatenate([block(e), block(f)], axis=1)
                rhs = jnp.concatenate([self.buf[at], self.buf[at + 1]], axis=1)
                found.append(
                    ((e >> 9) & 63, lax.dot_general(lhs, rhs, NT, preferred_element_type=F32))
                )
            for r, product in found:
                acc_ref[r] = acc_ref[r] + product
            return 0

        lax.fori_loop(0, self.groups, step, 0)


def local_kernel(list_ref, ends_ref, x_ref, vals_ref, acc_ref, buf, sems):
    tiles = Tiles(0, ends_ref[0], list_ref, vals_ref, buf, sems)
    tiles.begin()
    acc_ref[...] = jnp.zeros_like(acc_ref)

    def block(e):
        c = jnp.maximum((e >> 15) - 1, 0)
        x = x_ref[:, pl.ds(pl.multiple_of(c * 128, 128), 128)]
        return jnp.where(e > 0, x, jnp.zeros_like(x))

    tiles.add(block, acc_ref)


def remote_kernel(z_ref, list_ref, ends_ref, count_ref, sum_ref, far_ref, vals_ref, *rest):
    out_refs, (acc_ref, sum_buf, far_buf, sum_sem, far_sem, buf, sems) = rest[:4], rest[4:]
    parts = far_ref.shape[0]
    far_copy = pltpu.make_async_copy(far_ref, far_buf.at[pl.ds(1, parts)], far_sem)
    far_copy.start()
    tiles = Tiles(ends_ref[0], ends_ref[1], list_ref, vals_ref, buf, sems)
    tiles.begin()
    sum_copy = pltpu.make_async_copy(sum_ref, sum_buf, sum_sem)
    sum_copy.start()
    acc_ref[...] = jnp.zeros_like(acc_ref)
    far_buf[0] = jnp.zeros_like(far_buf[0])
    lane = lax.broadcasted_iota(I32, far_buf.shape[1:], 1)
    far_copy.wait()

    def clear(q, _):
        x = far_buf[q + 1]
        far_buf[q + 1] = jnp.where(lane < count_ref[q], x, jnp.zeros_like(x))
        return 0

    lax.fori_loop(0, parts, clear, 0, unroll=4)
    tiles.add(lambda e: far_buf[e >> 15], acc_ref)
    sum_copy.wait()
    z = z_ref[0]
    for k, out_ref in enumerate(out_refs):
        first = ((z + k) & 3) * 16
        for r in range(16):
            out_ref[r] = (acc_ref[first + r] + sum_buf[first + r]).astype(BF)


def project_kernel(z_ref, a_ref, b_ref, c_ref, d_ref, weight_ref, bias_ref, out_ref, w_ref):
    z = z_ref[0]
    for k in range(4):
        first = pl.multiple_of(((z - k) & 3) * 64, 64)
        w_ref[64 * k : 64 * k + 64, :] = weight_ref[pl.ds(first, 64), :]
    w = w_ref[...]
    for r in range(a_ref.shape[0]):
        x = jnp.concatenate([a_ref[r], b_ref[r], c_ref[r], d_ref[r]], axis=0)
        y = lax.dot_general(x, w, TN, preferred_element_type=F32) + bias_ref[...]
        out_ref[128 * r : 128 * r + 128, :] = jnp.maximum(y, 0.0).astype(BF)


def on_device(
    features, tile_vals, tile_row, tile_col, tile_count, recv_rows, recv_count, weight, bias
):
    width, v_rows = features.shape
    parts = recv_rows.shape[1]
    wanted = lax.all_to_all(recv_rows[0], "vert", split_axis=0, concat_axis=0, tiled=True)

    entries, ends = tile_lists(tile_row[0], tile_col[0], tile_count[0])
    table = pl.pallas_call(
        table_kernel,
        out_shape=jax.ShapeDtypeStruct((v_rows // 2, 128), F32),
        in_specs=[VMEM],
        out_specs=VMEM,
        compiler_params=params(8),
        cost_estimate=cost(10**7, 5 * 2**20),
        name="table",
    )(features)

    outgoing = pl.pallas_call(
        gather_kernel,
        out_shape=jax.ShapeDtypeStruct((parts, width, 128), BF),
        in_specs=[SMEM, VMEM, VMEM],
        out_specs=HBM,
        scratch_shapes=[
            pltpu.VMEM((128, 128), F32),
            pltpu.VMEM((parts, width, 128), BF),
            pltpu.SemaphoreType.DMA,
        ],
        compiler_params=params(57),
        cost_estimate=cost(10**7, 5 * 2**20),
        name="gather",
    )(wanted, wanted.reshape(parts, 1, 128), table.reshape(v_rows // 2, 1, 128))

    far = lax.all_to_all(outgoing, "vert", split_axis=0, concat_axis=0, tiled=True)

    acc = jax.ShapeDtypeStruct((v_rows // 128, width, 128), F32)
    ring = [pltpu.VMEM((DEPTH * 2 * U, 128, 128), BF), pltpu.SemaphoreType.DMA((DEPTH,))]
    local = pl.pallas_call(
        local_kernel,
        out_shape=acc,
        in_specs=[SMEM, SMEM, VMEM, HBM],
        out_specs=VMEM,
        scratch_shapes=ring,
        compiler_params=params(56),
        cost_estimate=cost(8 * 10**8, 20 * 2**20),
        name="local_tiles",
    )(entries, ends, features, tile_vals)

    z = lax.axis_index("feat").astype(I32)[None]
    piece = jax.ShapeDtypeStruct((16, width, 128), BF)
    pieces = pl.pallas_call(
        remote_kernel,
        out_shape=(piece,) * 4,
        in_specs=[SMEM, SMEM, SMEM, SMEM, HBM, HBM, HBM],
        out_specs=(VMEM,) * 4,
        scratch_shapes=[
            pltpu.VMEM(acc.shape, F32),
            pltpu.VMEM(acc.shape, F32),
            pltpu.VMEM((parts + 1, width, 128), BF),
            pltpu.SemaphoreType.DMA,
            pltpu.SemaphoreType.DMA,
        ]
        + ring,
        compiler_params=params(54),
        cost_estimate=cost(4 * 10**8, 20 * 2**20),
        name="remote_tiles",
    )(z, entries, ends, recv_count[0], local, far, tile_vals)

    def move(x, k):
        return lax.ppermute(x, "feat", [(i, (i + k) % 4) for i in range(4)])

    moved = [pieces[0]] + [None] * 3
    for k in (2, 1, 3):
        moved[k] = move(pieces[k], k)

    return pl.pallas_call(
        project_kernel,
        out_shape=jax.ShapeDtypeStruct((v_rows // 4, weight.shape[1]), BF),
        in_specs=[SMEM] + [VMEM] * 6,
        out_specs=VMEM,
        scratch_shapes=[pltpu.VMEM(weight.shape, BF)],
        compiler_params=params(6),
        cost_estimate=cost(3 * 10**8, 3 * 2**20),
        name="project",
    )(z, *moved, weight, bias[None, :])


def solution(mesh):
    in_specs = (
        P("feat", "vert"),
        P("vert", None, None),
        P("vert", None),
        P("vert", None),
        P("vert"),
        P("vert", None, None),
        P("vert", None),
        P(),
        P(),
    )
    out_specs = P(("vert", "feat"), None)
    return jax.shard_map(
        on_device, mesh=mesh, in_specs=in_specs, out_specs=out_specs, check_vma=False
    )
```

time: 116 us -> 71.8 us (0.62)
  matrix products: 32.1 us -> 0 us
  local copies, waits for them, and re-layouts: 33.8 us -> 4.9 us
  Pallas kernels: 0 us -> 24.8 us
  blocking collectives: 19.7 us -> 0 us
  starting transfers between devices: 12.9 us -> 21.7 us
  other arithmetic: 0.65 us -> 3.53 us
  waiting for transfers between devices: 15.8 us -> 13.9 us
  between operations: 0.78 us -> 2.61 us
    dot_general x4 -> x0, matrix products: 32.1 us -> none  [the longest x1 17.3 us: on_device(): jnp.einsum('ftj,tij->tfi', blocks, tile_vals, preferred_element_type=jnp....]
    gather x2 -> x0, local copies, waits for them, and re-layouts: 28.5 us -> none  [the longest x1 15 us: on_device(): outgoing = features[:, wanted.reshape(-1)].reshape(width, parts, slots)]
    pallas_call x0 -> x5, Pallas kernels: none -> 24.8 us  [the longest x1 9.07 us: on_device(): pl.pallas_call(gather_kernel, out_shape=jax.ShapeDtypeStruct((parts, widt...]
    all_to_all x1 -> x0, blocking collectives: 19.7 us -> none  [on_device(): lax.all_to_all(aggregate, 'feat', split_axis=1, concat_axis=0, tiled=True)]
    all_to_all x2, waiting for transfers between devices: 15.8 us -> 2.27 us  [the longest x1 2.27 us: on_device(): lax.all_to_all(outgoing, 'vert', split_axis=0, concat_axis=0, tiled=True)]
    ppermute x0 -> x3, waiting for transfers between devices: none -> 11.6 us  [move(): return lax.ppermute(x, 'feat', [(i, (i + k) % 4) for i in range(4)])]
    ppermute x0 -> x3, starting transfers between devices: none -> 5.74 us  [move(): return lax.ppermute(x, 'feat', [(i, (i + k) % 4) for i in range(4)])]
    all_to_all x2, starting transfers between devices: 12.9 us -> 16 us  [the longest x1 8.58 us: on_device(): lax.all_to_all(recv_rows[0], 'vert', split_axis=0, concat_axis=0, tiled=T...]
  transfers between devices with their start and end apart: 2 -> 5, of which waited for: 2 -> 3; matrix products, arithmetic and copies ran while one was open for 2% -> 5% of each run, Pallas kernels for 0% -> 12%
where the time goes in v1:
time: 71.8 us; the launch traced here: 71.5 us
  Pallas kernels  24.8 us (35%)
  starting transfers between devices  21.7 us (30%)
  waiting for transfers between devices  13.9 us (19%)
  local copies, waits for them, and re-layouts  4.9 us (7%)
  other arithmetic  3.53 us (5%)
  between operations  2.61 us (4%)
    ppermute x3, waiting for transfers between devices, move(): return lax.ppermute(x, 'feat', [(i, (i + k) % 4) for i in range(4)])  11.6 us
    pallas_call x1, Pallas kernels, on_device(): pl.pallas_call(gather_kernel, out_shape=jax.ShapeDtypeStruct((parts, widt...  9.07 us
    all_to_all x1, starting transfers between devices, on_device(): lax.all_to_all(recv_rows[0], 'vert', split_axis=0, concat_axis=0, tiled=T...  8.58 us
    pallas_call x1, Pallas kernels, on_device(): pl.pallas_call(local_kernel, out_shape=acc, in_specs=[SMEM, SMEM, VMEM, H...  7.82 us
    all_to_all x1, starting transfers between devices, on_device(): lax.all_to_all(outgoing, 'vert', split_axis=0, concat_axis=0, tiled=True)  7.4 us
    ppermute x3, starting transfers between devices, move(): return lax.ppermute(x, 'feat', [(i, (i + k) % 4) for i in range(4)])  5.74 us
    pallas_call x1, Pallas kernels, on_device(): pl.pallas_call(remote_kernel, out_shape=(piece,) * 4, in_specs=[SMEM, SME...  5.6 us
    unnamed x14, local copies, waits for them, and re-layouts  4.9 us
  transfers between devices with their start and end apart: 5, of which 3 were waited for; matrix products, arithmetic and copies ran while one was open for 5% of the time, Pallas kernels for 12%

profile of v1, /device:TPU:1, one launch (start us, length us, event | category | flops | bytes accessed | tf_op | source)
XLA Modules:
  0.0 71.5 jit_solution(10470548351914667977)
XLA Ops:
  0.0 8.6 %all-to-all-start = ((s32[32,1,128]{2,1,0:T(1,128)}), s32[32,1,128]{2,1,0:T(1,128)S(1)}, u32[]{:S(2)}, u32[]{:S(2)}) async-start(s32[32,1,128]{2,1,0:T(1,128)} %bitcast.22), calls=%async_computation | async-start | bytes 32768 | tf_op jit(solution)/shard_map/all_to_all | solution.py:184
  9.2 0.7 compare_select_fusion.2
  9.9 0.1 convert_reduce_fusion.1
  10.1 0.7 %select_reduce_fusion.3 = (s32[]{:T(128)}, s32[]{:T(128)}, s32[128]{0:T(128)S(1)}) fusion(s32[128]{0:T(128)S(1)} %convert_reduce_fusion.1), kind=kLoop, calls=%fused_computation.23 | loop fusion | flops 2686 | bytes 1032 | tf_op jit(solution)/shard_map/reduce_sum | solution.py:37
  11.9 0.1 select_reduce_fusion.2
  12.1 0.1 select_reduce_fusion.1
  12.2 0.2 convert_reduce_fusion
  13.1 0.0 copy-start.1
  13.2 1.2 %copy-done.1 = bf16[64,8192]{1,0:T(8,128)(2,1)S(1)} copy-done((bf16[64,8192]{1,0:T(8,128)(2,1)S(1)}, bf16[64,8192]{1,0:T(8,128)(2,1)}, u32[]{:S(2)}) %copy-start.1) | copy-done | bytes 1048600
  14.4 0.9 %table.1 = f32[4096,128]{1,0:T(8,128)S(1)} custom-call(bf16[64,8192]{1,0:T(8,128)(2,1)S(1)} %copy-done.1), custom_call_target="tpu_custom_call" | custom-call | flops 10000000 | bytes 5242880 | tf_op jit(solution)/shard_map/table/pallas_call | solution.py:187
  15.3 0.0 copy-start
  15.3 1.3 %copy-done = f32[4096,128]{1,0:T(8,128)} copy-done((f32[4096,128]{1,0:T(8,128)}, f32[4096,128]{1,0:T(8,128)S(1)}, u32[]{:S(2)}) %copy-start) | copy-done | bytes 2097176
  16.6 0.0 all-to-all-done.which_ref
  16.6 0.0 copy-start.6
  16.6 0.6 copy-done.6
  17.2 9.1 %gather.1 = bf16[32,64,128]{2,1,0:T(8,128)(2,1)} custom-call(s32[32,128]{1,0:T(8,128)} %bitcast.18, s32[32,1,128]{2,1,0:T(1,128)} %copy-done.6, f32[4096,1,128]{2,1,0:T(1,128)} %bitcast.16), custom_call_target="tpu_custom_call" | custom-call | flops 10000000 | bytes 5242880 | tf_op jit(solution)/shard_map/gather/pallas_call | solution.py:197
  26.3 7.4 %all-to-all-start.1 = ((bf16[32,64,128]{2,1,0:T(8,128)(2,1)}), bf16[32,64,128]{2,1,0:T(8,128)(2,1)S(1)}, u32[]{:S(2)}, u32[]{:S(2)}) async-start(bf16[32,64,128]{2,1,0:T(8,128)(2,1)} %gather.1), calls=%async_computation.1 | async-start | bytes 1048576 | tf_op jit(solution)/shard_map/all_to_all | solution.py:212
  33.7 0.7 pad_add_fusion.ends_ref
  34.4 0.8 %select_reduce_fusion.list_ref = s32[672]{0:T(1024)} fusion(s32[512]{0:T(512)S(1)} %bitcast.26, s32[512]{0:T(512)S(1)} %bitcast.24), kind=kLoop, calls=%fused_computation | loop fusion | flops 1031520 | bytes 6784 | tf_op jit(solution)/shard_map/reduce_sum | solution.py:46
  35.2 7.8 %local_tiles.1.sum_ref = f32[64,64,128]{2,1,0:T(8,128)} custom-call(s32[672]{0:T(1024)} %select_reduce_fusion.list_ref, s32[2]{0:T(128)} %pad_add_fusion.ends_ref, bf16[64,8192]{1,0:T(8,128)(2,1)} %x_ref.3, bf16[512,128,128]{2,1,0:T(8,128)(2,1)} %vals_ref.3), custom_call_target="tpu_custom_call" | custom-call | flops 800000000 | bytes 20971520 | tf_op jit(solution)/shard_map/local_tiles/pallas_call | solution.py:216
  43.0 2.3 %all-to-all-done.1.far_ref = bf16[32,64,128]{2,1,0:T(8,128)(2,1)S(1)} async-done(((bf16[32,64,128]{2,1,0:T(8,128)(2,1)}), bf16[32,64,128]{2,1,0:T(8,128)(2,1)S(1)}, u32[]{:S(2)}, u32[]{:S(2)}) %all-to-all-start.1) | async-done | bytes 524320 | tf_op jit(solution)/shard_map/all_to_all | solution.py:212
  45.3 0.0 copy-start.5
  45.3 0.8 %copy-done.5 = bf16[32,64,128]{2,1,0:T(8,128)(2,1)} copy-done((bf16[32,64,128]{2,1,0:T(8,128)(2,1)}, bf16[32,64,128]{2,1,0:T(8,128)(2,1)S(1)}, u32[]{:S(2)}) %copy-start.5) | copy-done | bytes 524312
  46.1 0.0 copy-start.3
  46.1 0.0 copy-start.4
  46.1 5.6 %remote_tiles.1 = (bf16[16,64,128]{2,1,0:T(8,128)(2,1)}, bf16[16,64,128]{2,1,0:T(8,128)(2,1)}, bf16[16,64,128]{2,1,0:T(8,128)(2,1)}, bf16[16,64,128]{2,1,0:T(8,128)(2,1)}) custom-call(s32[1]{0:T(128)} %bitcast.z_ref, s32[672]{0:T(1024)} %select_reduce_fusion.list_ref, s32[2]{0:T(128)} %pad_add_fusion.ends_ref, s32[32]{0:T(128)} %bitcast.27, ...), custom_call_target="tpu_custom_call" | custom-call | flops 400000000 | bytes 20971520 | tf_op jit(solution)/shard_map/remote_tiles/pallas_call | solution.py:229
  51.7 1.7 %collective-permute-start = (bf16[16,64,128]{2,1,0:T(8,128)(2,1)}, bf16[16,64,128]{2,1,0:T(8,128)(2,1)S(1)}, u32[]{:S(2)}, u32[]{:S(2)}) collective-permute-start(bf16[16,64,128]{2,1,0:T(8,128)(2,1)} %get-tuple-element.10), channel_id=1, source_target_pairs={{0,1},{1,2},{2,3},{3,0},{4,5},{5,6},{6,7},{7,4},{8,9},{9,10},{10,1... | collective-permute-start | bytes 786440 | tf_op jit(solution)/shard_map/ppermute | solution.py:248
  53.4 3.3 %collective-permute-start.1 = (bf16[16,64,128]{2,1,0:T(8,128)(2,1)}, bf16[16,64,128]{2,1,0:T(8,128)(2,1)S(1)}, u32[]{:S(2)}, u32[]{:S(2)}) collective-permute-start(bf16[16,64,128]{2,1,0:T(8,128)(2,1)} %get-tuple-element.11), channel_id=1, source_target_pairs={{0,2},{1,3},{2,0},{3,1},{4,6},{5,7},{6,4},{7,5},{8,10},{9,11},{10,... | collective-permute-start | bytes 786440 | tf_op jit(solution)/shard_map/ppermute | solution.py:248
  56.7 0.7 %collective-permute-start.2 = (bf16[16,64,128]{2,1,0:T(8,128)(2,1)}, bf16[16,64,128]{2,1,0:T(8,128)(2,1)S(1)}, u32[]{:S(2)}, u32[]{:S(2)}) collective-permute-start(bf16[16,64,128]{2,1,0:T(8,128)(2,1)} %get-tuple-element.12), channel_id=1, source_target_pairs={{0,3},{1,0},{2,1},{3,2},{4,7},{5,4},{6,5},{7,6},{8,11},{9,8},{10,9... | collective-permute-start | bytes 786440 | tf_op jit(solution)/shard_map/ppermute | solution.py:248
  57.4 5.1 %collective-permute-done.b_ref = bf16[16,64,128]{2,1,0:T(8,128)(2,1)S(1)} collective-permute-done((bf16[16,64,128]{2,1,0:T(8,128)(2,1)}, bf16[16,64,128]{2,1,0:T(8,128)(2,1)S(1)}, u32[]{:S(2)}, u32[]{:S(2)}) %collective-permute-start) | collective-permute-done | bytes 262176 | tf_op jit(solution)/shard_map/ppermute | solution.py:248
  62.5 6.5 %collective-permute-done.1.c_ref = bf16[16,64,128]{2,1,0:T(8,128)(2,1)S(1)} collective-permute-done((bf16[16,64,128]{2,1,0:T(8,128)(2,1)}, bf16[16,64,128]{2,1,0:T(8,128)(2,1)S(1)}, u32[]{:S(2)}, u32[]{:S(2)}) %collective-permute-start.1) | collective-permute-done | bytes 262176 | tf_op jit(solution)/shard_map/ppermute | solution.py:248
  69.0 0.0 collective-permute-done.2.d_ref
  69.1 0.0 copy-done.3
  69.1 0.0 copy-done.4
  69.1 0.0 copy-start.2
  69.1 0.9 %copy-done.2 = bf16[16,64,128]{2,1,0:T(8,128)(2,1)S(1)} copy-done((bf16[16,64,128]{2,1,0:T(8,128)(2,1)S(1)}, bf16[16,64,128]{2,1,0:T(8,128)(2,1)}, u32[]{:S(2)}) %copy-start.2) | copy-done | bytes 262168
  70.0 1.5 %project.1 = bf16[2048,256]{1,0:T(8,128)(2,1)} custom-call(s32[1]{0:T(128)} %bitcast.z_ref, bf16[16,64,128]{2,1,0:T(8,128)(2,1)S(1)} %copy-done.2, bf16[16,64,128]{2,1,0:T(8,128)(2,1)S(1)} %collective-permute-done.b_ref, bf16[16,64,128]{2,1,0:T(8,128)(2,1)S(1)} %collective-permute-done.1.c_ref, bf16[16,64,128]{2,1,0:T(8,128)(2,1)S(1)} %collective-permute-done.2.d_ref, ...), custom_call_target="tpu_custom_call" | custom-call | flops 300000000 | bytes 3145728 | tf_op jit(solution)/shard_map/project/pallas_call | solution.py:254
  (4 shorter events, 0.0 us)
Async XLA Ops:
  0.0 16.6 %all-to-all-start = ((s32[32,1,128]{2,1,0:T(1,128)}), s32[32,1,128]{2,1,0:T(1,128)S(1)}, u32[]{:S(2)}, u32[]{:S(2)}) async-start(s32[32,1,128]{2,1,0:T(1,128)} %bitcast.22), calls=%async_computation | async-start | bytes 32768 | tf_op jit(solution)/shard_map/all_to_all | solution.py:184
  13.1 1.2 %copy-start.1 = (bf16[64,8192]{1,0:T(8,128)(2,1)S(1)}, bf16[64,8192]{1,0:T(8,128)(2,1)}, u32[]{:S(2)}) copy-start(bf16[64,8192]{1,0:T(8,128)(2,1)} %x_ref.3) | copy-start | bytes 3145732
  15.3 1.4 %copy-start = (f32[4096,128]{1,0:T(8,128)}, f32[4096,128]{1,0:T(8,128)S(1)}, u32[]{:S(2)}) copy-start(f32[4096,128]{1,0:T(8,128)S(1)} %table.1) | copy-start | bytes 6291460
  16.6 0.6 copy-start.6
  26.3 19.0 %all-to-all-start.1 = ((bf16[32,64,128]{2,1,0:T(8,128)(2,1)}), bf16[32,64,128]{2,1,0:T(8,128)(2,1)S(1)}, u32[]{:S(2)}, u32[]{:S(2)}) async-start(bf16[32,64,128]{2,1,0:T(8,128)(2,1)} %gather.1), calls=%async_computation.1 | async-start | bytes 1048576 | tf_op jit(solution)/shard_map/all_to_all | solution.py:212
  45.3 0.8 %copy-start.5 = (bf16[32,64,128]{2,1,0:T(8,128)(2,1)}, bf16[32,64,128]{2,1,0:T(8,128)(2,1)S(1)}, u32[]{:S(2)}) copy-start(bf16[32,64,128]{2,1,0:T(8,128)(2,1)S(1)} %all-to-all-done.1.far_ref) | copy-start | bytes 1572868
  46.1 23.0 %copy-start.3 = (bf16[256,256]{1,0:T(8,128)(2,1)S(1)}, bf16[256,256]{1,0:T(8,128)(2,1)}, u32[]{:S(2)}) copy-start(bf16[256,256]{1,0:T(8,128)(2,1)} %weight_ref.1) | copy-start | bytes 393220
  46.1 23.0 %copy-start.4 = (f32[256]{0:T(256)S(1)}, f32[256]{0:T(256)}, u32[]{:S(2)}) copy-start(f32[256]{0:T(256)} %param.17) | copy-start | bytes 3076
  51.7 10.8 %collective-permute-start = (bf16[16,64,128]{2,1,0:T(8,128)(2,1)}, bf16[16,64,128]{2,1,0:T(8,128)(2,1)S(1)}, u32[]{:S(2)}, u32[]{:S(2)}) collective-permute-start(bf16[16,64,128]{2,1,0:T(8,128)(2,1)} %get-tuple-element.10), channel_id=1, source_target_pairs={{0,1},{1,2},{2,3},{3,0},{4,5},{5,6},{6,7},{7,4},{8,9},{9,10},{10,1... | collective-permute-start | bytes 786440 | tf_op jit(solution)/shard_map/ppermute | solution.py:248
  53.4 15.7 %collective-permute-start.1 = (bf16[16,64,128]{2,1,0:T(8,128)(2,1)}, bf16[16,64,128]{2,1,0:T(8,128)(2,1)S(1)}, u32[]{:S(2)}, u32[]{:S(2)}) collective-permute-start(bf16[16,64,128]{2,1,0:T(8,128)(2,1)} %get-tuple-element.11), channel_id=1, source_target_pairs={{0,2},{1,3},{2,0},{3,1},{4,6},{5,7},{6,4},{7,5},{8,10},{9,11},{10,... | collective-permute-start | bytes 786440 | tf_op jit(solution)/shard_map/ppermute | solution.py:248
  56.7 12.4 %collective-permute-start.2 = (bf16[16,64,128]{2,1,0:T(8,128)(2,1)}, bf16[16,64,128]{2,1,0:T(8,128)(2,1)S(1)}, u32[]{:S(2)}, u32[]{:S(2)}) collective-permute-start(bf16[16,64,128]{2,1,0:T(8,128)(2,1)} %get-tuple-element.12), channel_id=1, source_target_pairs={{0,3},{1,0},{2,1},{3,2},{4,7},{5,4},{6,5},{7,6},{8,11},{9,8},{10,9... | collective-permute-start | bytes 786440 | tf_op jit(solution)/shard_map/ppermute | solution.py:248
  69.1 1.0 %copy-start.2 = (bf16[16,64,128]{2,1,0:T(8,128)(2,1)S(1)}, bf16[16,64,128]{2,1,0:T(8,128)(2,1)}, u32[]{:S(2)}) copy-start(bf16[16,64,128]{2,1,0:T(8,128)(2,1)} %get-tuple-element.9.a_ref) | copy-start | bytes 786436

commit v2 on v1

v2 whole, which is shorter than its diff:
```python
import jax
import jax.numpy as jnp
from jax import lax
from jax.experimental import pallas as pl
from jax.experimental.pallas import tpu as pltpu
from jax.sharding import PartitionSpec as P

LOG_U = 4
U = 1 << LOG_U
LOG_V = 4
V = 1 << LOG_V
W = 4
NT = (((1,), (1,)), ((), ()))
TN = (((0,), (0,)), ((), ()))
VMEM = pl.BlockSpec(memory_space=pltpu.VMEM)
HBM = pl.BlockSpec(memory_space=pltpu.HBM)
SMEM = pl.BlockSpec(memory_space=pltpu.SMEM)
BF, F32, I32 = jnp.bfloat16, jnp.float32, jnp.int32


def params(mib):
    return pltpu.CompilerParams(vmem_limit_bytes=mib << 20)


def cost(flops, nbytes):
    return pl.CostEstimate(flops=flops, bytes_accessed=nbytes, transcendentals=0)


def prepare_kernel(
    count_ref, row_ref, col_ref, x_ref, table_ref, order_ref, list_ref, ends_ref
):
    half = table_ref.shape[0]

    def turn(k, _):
        at = pl.multiple_of(k * 128, 128)
        x = jnp.concatenate([x_ref[:, pl.ds(at, 128)], x_ref[:, pl.ds(at + half, 128)]], axis=0)
        table_ref[pl.ds(at, 128), :] = x.astype(F32).T
        return 0

    lax.fori_loop(0, half // 128, turn, 0, unroll=4)

    n = row_ref.shape[1]

    def columns(*rows):
        x = jnp.concatenate(list(rows) + [rows[0]] * (8 - len(rows)), axis=0).T
        return [x[:, k : k + 1] for k in range(len(rows))]

    def total(x):
        return jnp.sum(x, axis=1, keepdims=True)

    def count(x):
        return jnp.sum(jnp.where(x, 1.0, 0.0), axis=0, keepdims=True)

    t = lax.broadcasted_iota(I32, (1, n), 1)
    row, col = row_ref[...], col_ref[...]
    is_far = col >= 64
    used = t < count_ref[0]
    key = jnp.where(used, row + jnp.where(is_far, 64, 0), 128).astype(F32)
    (key_c,) = columns(key)
    t_c = lax.broadcasted_iota(I32, (n, 1), 0)
    less = key_c < key
    place = count((key_c == key) & (t_c < t))
    even = (place.astype(I32) & 1) == 0
    (even_c,) = columns(jnp.where(even, 1.0, 0.0))
    rank = count(less) + place
    before = jnp.sum(jnp.where(less, even_c, 0.0), axis=0, keepdims=True)
    near, far = used & ~is_far, used & is_far
    near_tiles = total(jnp.where(near, 1.0, 0.0)).astype(I32)
    used_tiles = total(jnp.where(used, 1.0, 0.0)).astype(I32)
    near_pairs = total(jnp.where(near & even, 1.0, 0.0)).astype(I32)
    far_pairs = total(jnp.where(far & even, 1.0, 0.0)).astype(I32)
    near_groups = (near_pairs + (U - 1)) >> LOG_U
    far_groups = (far_pairs + (U - 1)) >> LOG_U
    rank_i = rank.astype(I32)
    fill = jnp.where(is_far, near_groups * U - near_pairs, 0)
    slot = 2 * (before.astype(I32) + fill) + place.astype(I32)
    own = rank_i - jnp.where(is_far, near_tiles, 0)
    entry = own | (row << 9) | ((jnp.where(is_far, col - 64, col) + 1) << 15)
    rank_c, slot_c, entry_c = columns(
        jnp.where(used, rank, -1.0),
        jnp.where(used, slot, -1).astype(F32),
        jnp.where(used, entry, 0).astype(F32),
    )
    r = lax.broadcasted_iota(I32, (1, order_ref.shape[1]), 1).astype(F32)
    order = jnp.where(rank_c == r, t_c.astype(F32), 0.0)
    order_ref[...] = jnp.sum(order, axis=0, keepdims=True).astype(I32)
    s = lax.broadcasted_iota(I32, (1, list_ref.shape[1]), 1).astype(F32)
    entries = jnp.where(slot_c == s, entry_c, 0.0)
    list_ref[...] = jnp.sum(entries, axis=0, keepdims=True).astype(I32)
    lane = lax.broadcasted_iota(I32, (1, 128), 1)
    ends = jnp.where(lane == 0, near_tiles, used_tiles)
    ends = jnp.where(lane == 2, near_groups, ends)
    ends_ref[...] = jnp.where(lane == 3, far_groups, ends)


def gather_kernel(idx_ref, which_ref, table_ref, out_ref, even_ref, odd_ref, buf, sem):
    half = table_ref.shape[0]
    parts = out_ref.shape[0]

    def fill(p, rows_ref):
        own = [idx_ref.at[p + k] for k in range(W)]
        for s in range(128):
            for k in range(W):
                rows_ref[128 * k + s : 128 * k + s + 1, :] = table_ref[own[k][s] & (half - 1)]

    def turn(p, rows_ref):
        for k in range(W):
            g = rows_ref[128 * k : 128 * k + 128, :].T
            buf[p + k] = jnp.where(which_ref[p + k] < half, g[:64], g[64:]).astype(BF)

    def send(p, n):
        some = pl.ds(p, n)
        pltpu.make_async_copy(buf.at[some], out_ref.at[some], sem).start()

    def step(m, _):
        fill(2 * W * m, even_ref)
        turn(jnp.maximum(2 * W * m - W, 0), odd_ref)
        fill(2 * W * m + W, odd_ref)
        turn(2 * W * m, even_ref)

        @pl.when(m > 0)
        def _():
            send(2 * W * (m - 1), 2 * W)

        return 0

    lax.fori_loop(0, parts // (2 * W), step, 0)
    turn(parts - W, odd_ref)
    send(parts - 2 * W, 2 * W)
    pltpu.make_async_copy(buf, out_ref, sem).wait()


def bring(first, n, order_ref, vals_ref, buf, sems):
    def step(c, _):
        for k in range(V):
            i = c * V + k
            pltpu.make_async_copy(
                vals_ref.at[order_ref[0, first + i]], buf.at[i], sems.at[c]
            ).start()
        return 0

    lax.fori_loop(0, (n + (V - 1)) >> LOG_V, step, 0)


def add_pairs(first, groups, n, list_ref, block, vals_ref, buf, sems, acc_ref):
    chunks = (n + (V - 1)) >> LOG_V

    def wait(c, _):
        here = pl.ds(pl.multiple_of(c * V, V), V)
        pltpu.make_async_copy(vals_ref.at[pl.ds(0, V)], buf.at[here], sems.at[c]).wait()
        return 0

    def step(c, ready):
        at = 2 * U * (first + c)
        top = jnp.maximum(list_ref[0, at + 2 * U - 2] & 511, list_ref[0, at + 2 * U - 1] & 511)
        need = jnp.where(c == groups - 1, chunks, (top >> LOG_V) + 1)
        lax.fori_loop(ready, need, wait, 0)
        found = []
        for u in range(U):
            e, f = list_ref[0, at + 2 * u], list_ref[0, at + 2 * u + 1]
            lhs = jnp.concatenate([block(e), block(f)], axis=1)
            rhs = jnp.concatenate([buf[e & 511], buf[f & 511]], axis=1)
            found.append(
                ((e >> 9) & 63, lax.dot_general(lhs, rhs, NT, preferred_element_type=F32))
            )
        for r, product in found:
            acc_ref[r] = acc_ref[r] + product
        return need

    lax.fori_loop(0, groups, step, 0)


def local_kernel(order_ref, list_ref, ends_ref, x_ref, vals_ref, acc_ref, buf, sems):
    n = ends_ref[0, 0]
    bring(0, n, order_ref, vals_ref, buf, sems)
    acc_ref[...] = jnp.zeros_like(acc_ref)

    def block(e):
        c = jnp.maximum((e >> 15) - 1, 0)
        x = x_ref[:, pl.ds(pl.multiple_of(c * 128, 128), 128)]
        return jnp.where(e > 0, x, jnp.zeros_like(x))

    add_pairs(0, ends_ref[0, 2], n, list_ref, block, vals_ref, buf, sems, acc_ref)


def remote_kernel(
    z_ref, order_ref, list_ref, ends_ref, count_ref, sum_ref, far_ref, vals_ref, *rest
):
    out_refs, (acc_ref, sum_buf, far_buf, sum_sem, buf, sems) = rest[:4], rest[4:]
    n = ends_ref[0, 1] - ends_ref[0, 0]
    bring(ends_ref[0, 0], n, order_ref, vals_ref, buf, sems)
    sum_copy = pltpu.make_async_copy(sum_ref, sum_buf, sum_sem)
    sum_copy.start()
    acc_ref[...] = jnp.zeros_like(acc_ref)
    far_buf[0] = jnp.zeros_like(far_buf[0])
    lane = lax.broadcasted_iota(I32, far_buf.shape[1:], 1)

    def clear(q, _):
        x = far_ref[q]
        far_buf[q + 1] = jnp.where(lane < count_ref[q], x, jnp.zeros_like(x))
        return 0

    lax.fori_loop(0, far_ref.shape[0], clear, 0, unroll=4)
    add_pairs(
        ends_ref[0, 2],
        ends_ref[0, 3],
        n,
        list_ref,
        lambda e: far_buf[e >> 15],
        vals_ref,
        buf,
        sems,
        acc_ref,
    )
    sum_copy.wait()
    z = z_ref[0]
    for k, out_ref in enumerate(out_refs):
        first = ((z + k) & 3) * 16
        for r in range(16):
            out_ref[r] = (acc_ref[first + r] + sum_buf[first + r]).astype(BF)


def project_kernel(z_ref, a_ref, b_ref, c_ref, d_ref, weight_ref, bias_ref, out_ref, w_ref):
    z = z_ref[0]
    for k in range(4):
        first = pl.multiple_of(((z - k) & 3) * 64, 64)
        w_ref[64 * k : 64 * k + 64, :] = weight_ref[pl.ds(first, 64), :]
    w = w_ref[...]
    for r in range(a_ref.shape[0]):
        x = jnp.concatenate([a_ref[r], b_ref[r], c_ref[r], d_ref[r]], axis=0)
        y = lax.dot_general(x, w, TN, preferred_element_type=F32) + bias_ref[...]
        out_ref[128 * r : 128 * r + 128, :] = jnp.maximum(y, 0.0).astype(BF)


def on_device(
    features, tile_vals, tile_row, tile_col, tile_count, recv_rows, recv_count, weight, bias
):
    width, v_rows = features.shape
    parts = recv_rows.shape[1]
    wanted = lax.all_to_all(recv_rows[0], "vert", split_axis=0, concat_axis=0, tiled=True)

    n_tiles = tile_vals.shape[0]
    table, order, entries, ends = pl.pallas_call(
        prepare_kernel,
        out_shape=(
            jax.ShapeDtypeStruct((v_rows // 2, 128), F32),
            jax.ShapeDtypeStruct((1, n_tiles + 128), I32),
            jax.ShapeDtypeStruct((1, n_tiles + 128 + 128), I32),
            jax.ShapeDtypeStruct((1, 128), I32),
        ),
        in_specs=[SMEM, VMEM, VMEM, VMEM],
        out_specs=(VMEM,) * 4,
        compiler_params=params(8),
        cost_estimate=cost(10**7, 5 * 2**20),
        name="prepare",
    )(tile_count, tile_row, tile_col, features)

    outgoing = pl.pallas_call(
        gather_kernel,
        out_shape=jax.ShapeDtypeStruct((parts, width, 128), BF),
        in_specs=[SMEM, VMEM, VMEM],
        out_specs=HBM,
        scratch_shapes=[
            pltpu.VMEM((W * 128, 128), F32),
            pltpu.VMEM((W * 128, 128), F32),
            pltpu.VMEM((parts, width, 128), BF),
            pltpu.SemaphoreType.DMA,
        ],
        compiler_params=params(40),
        cost_estimate=cost(10**7, 5 * 2**20),
        name="gather",
    )(wanted, wanted.reshape(parts, 1, 128), table.reshape(v_rows // 2, 1, 128))

    far = lax.all_to_all(outgoing, "vert", split_axis=0, concat_axis=0, tiled=True)

    acc = jax.ShapeDtypeStruct((v_rows // 128, width, 128), F32)
    room = [
        pltpu.VMEM((n_tiles, 128, 128), BF),
        pltpu.SemaphoreType.DMA((n_tiles // V,)),
    ]
    local = pl.pallas_call(
        local_kernel,
        out_shape=acc,
        in_specs=[SMEM, SMEM, SMEM, VMEM, HBM],
        out_specs=VMEM,
        scratch_shapes=room,
        compiler_params=params(49),
        cost_estimate=cost(8 * 10**8, 20 * 2**20),
        name="local_tiles",
    )(order, entries, ends, features, tile_vals)

    z = lax.axis_index("feat").astype(I32)[None]
    piece = jax.ShapeDtypeStruct((16, width, 128), BF)
    pieces = pl.pallas_call(
        remote_kernel,
        out_shape=(piece,) * 4,
        in_specs=[SMEM, SMEM, SMEM, SMEM, SMEM, HBM, VMEM, HBM],
        out_specs=(VMEM,) * 4,
        scratch_shapes=[
            pltpu.VMEM(acc.shape, F32),
            pltpu.VMEM(acc.shape, F32),
            pltpu.VMEM((parts + 1, width, 128), BF),
            pltpu.SemaphoreType.DMA,
        ]
        + room,
        compiler_params=params(49),
        cost_estimate=cost(4 * 10**8, 20 * 2**20),
        name="remote_tiles",
    )(z, order, entries, ends, recv_count[0], local, far, tile_vals)

    def move(x, k):
        return lax.ppermute(x, "feat", [(i, (i + k) % 4) for i in range(4)])

    moved = [pieces[0]] + [None] * 3
    for k in (2, 1, 3):
        moved[k] = move(pieces[k], k)

    return pl.pallas_call(
        project_kernel,
        out_shape=jax.ShapeDtypeStruct((v_rows // 4, weight.shape[1]), BF),
        in_specs=[SMEM] + [VMEM] * 6,
        out_specs=VMEM,
        scratch_shapes=[pltpu.VMEM(weight.shape, BF)],
        compiler_params=params(6),
        cost_estimate=cost(3 * 10**8, 3 * 2**20),
        name="project",
    )(z, *moved, weight, bias[None, :])


def solution(mesh):
    in_specs = (
        P("feat", "vert"),
        P("vert", None, None),
        P("vert", None),
        P("vert", None),
        P("vert"),
        P("vert", None, None),
        P("vert", None),
        P(),
        P(),
    )
    out_specs = P(("vert", "feat"), None)
    return jax.shard_map(
        on_device, mesh=mesh, in_specs=in_specs, out_specs=out_specs, check_vma=False
    )
```

time: 71.8 us -> 63.4 us (0.88)
  Pallas kernels: 24.8 us -> 18.7 us
  waiting for transfers between devices: 13.9 us -> 19.7 us
  other arithmetic: 3.53 us -> 0 us
  between operations: 2.61 us -> 0.75 us
  starting transfers between devices: 21.7 us -> 20.1 us
  local copies, waits for them, and re-layouts: 4.9 us -> 3.39 us
    all_to_all x1, waiting for transfers between devices: 2.27 us -> 6.98 us  [on_device(): lax.all_to_all(outgoing, 'vert', split_axis=0, concat_axis=0, tiled=True)]
    pallas_call x1, Pallas kernels: 9.07 us -> 5.81 us  [on_device(): pl.pallas_call(gather_kernel, out_shape=jax.ShapeDtypeStruct((parts, widt...]
    reduce_sum x6 -> x0, other arithmetic: 2.12 us -> none  [the longest x1 0.81 us: tile_lists(): jnp.sum(jnp.where(slot[None, :] == s[:, None], entry[None, :], 0), axis=1)]
    pallas_call x2, Pallas kernels: 8.7 us -> 6.64 us  [the longest x1 4.63 us: on_device(): pl.pallas_call(local_kernel, out_shape=acc, in_specs=[SMEM, SMEM, SMEM, V...]
    all_to_all x1, waiting for transfers between devices: 0.01 us -> 1.62 us  [on_device(): lax.all_to_all(recv_rows[0], 'vert', split_axis=0, concat_axis=0, tiled=T...]
    all_to_all x1, starting transfers between devices: 7.4 us -> 5.83 us  [on_device(): lax.all_to_all(outgoing, 'vert', split_axis=0, concat_axis=0, tiled=True)]
    unnamed x14 -> x16, local copies, waits for them, and re-layouts: 4.9 us -> 3.39 us
    pallas_call x1, Pallas kernels: 5.6 us -> 4.76 us  [on_device(): pl.pallas_call(remote_kernel, out_shape=(piece,) * 4, in_specs=[SMEM, SME...]
  transfers between devices with their start and end apart: 5 -> 5, of which waited for: 3 -> 4; matrix products, arithmetic and copies ran while one was open for 5% -> 0% of each run, Pallas kernels for 12% -> 11%
where the time goes in v2:
time: 63.4 us; the launch traced here: 62.7 us
  starting transfers between devices  20.1 us (32%)
  waiting for transfers between devices  19.7 us (31%)
  Pallas kernels  18.7 us (29%)
  local copies, waits for them, and re-layouts  3.39 us (5%)
  between operations  0.75 us (1%)
    ppermute x3, waiting for transfers between devices, move(): return lax.ppermute(x, 'feat', [(i, (i + k) % 4) for i in range(4)])  11.1 us
    all_to_all x1, starting transfers between devices, on_device(): lax.all_to_all(recv_rows[0], 'vert', split_axis=0, concat_axis=0, tiled=T...  8.58 us
    all_to_all x1, waiting for transfers between devices, on_device(): lax.all_to_all(outgoing, 'vert', split_axis=0, concat_axis=0, tiled=True)  6.98 us
    all_to_all x1, starting transfers between devices, on_device(): lax.all_to_all(outgoing, 'vert', split_axis=0, concat_axis=0, tiled=True)  5.83 us
    pallas_call x1, Pallas kernels, on_device(): pl.pallas_call(gather_kernel, out_shape=jax.ShapeDtypeStruct((parts, widt...  5.81 us
    ppermute x3, starting transfers between devices, move(): return lax.ppermute(x, 'feat', [(i, (i + k) % 4) for i in range(4)])  5.73 us
    pallas_call x1, Pallas kernels, on_device(): pl.pallas_call(remote_kernel, out_shape=(piece,) * 4, in_specs=[SMEM, SME...  4.76 us
    pallas_call x1, Pallas kernels, on_device(): pl.pallas_call(local_kernel, out_shape=acc, in_specs=[SMEM, SMEM, SMEM, V...  4.63 us
  transfers between devices with their start and end apart: 5, of which 4 were waited for; matrix products, arithmetic and copies ran while one was open for 0% of the time, Pallas kernels for 11%

profile of v2, /device:TPU:1, one launch (start us, length us, event | category | flops | bytes accessed | tf_op | source)
XLA Modules:
  0.0 62.7 jit_solution(17885692614239058785)
XLA Ops:
  0.0 8.6 %all-to-all-start = ((s32[32,1,128]{2,1,0:T(1,128)}), s32[32,1,128]{2,1,0:T(1,128)S(1)}, u32[]{:S(2)}, u32[]{:S(2)}) async-start(s32[32,1,128]{2,1,0:T(1,128)} %bitcast.10), calls=%async_computation | async-start | bytes 32768 | tf_op jit(solution)/shard_map/all_to_all | solution.py:240
  9.2 0.0 copy-start
  9.2 1.2 %copy-done = bf16[64,8192]{1,0:T(8,128)(2,1)S(1)} copy-done((bf16[64,8192]{1,0:T(8,128)(2,1)S(1)}, bf16[64,8192]{1,0:T(8,128)(2,1)}, u32[]{:S(2)}) %copy-start) | copy-done | bytes 1048600
  10.5 0.0 copy-start.4
  10.5 0.7 %copy-done.4 = s32[1,512]{1,0:T(1,128)S(1)} copy-done((s32[1,512]{1,0:T(1,128)S(1)}, s32[1,512]{1,0:T(1,128)}, u32[]{:S(2)}) %copy-start.4) | copy-done | bytes 2072
  11.1 0.0 copy-start.5
  11.1 0.7 %copy-done.5 = s32[1,512]{1,0:T(1,128)S(1)} copy-done((s32[1,512]{1,0:T(1,128)S(1)}, s32[1,512]{1,0:T(1,128)}, u32[]{:S(2)}) %copy-start.5) | copy-done | bytes 2072
  11.8 2.0 %prepare.1 = (f32[4096,128]{1,0:T(8,128)S(1)}, s32[1,640]{1,0:T(1,128)S(1)}, s32[1,768]{1,0:T(1,128)S(1)}, s32[1,128]{1,0:T(1,128)S(1)}) custom-call(s32[1]{0:T(128)S(6)} %copy.10.count_ref, s32[1,512]{1,0:T(1,128)S(1)} %copy-done.4, s32[1,512]{1,0:T(1,128)S(1)} %copy-done.5, bf16[64,8192]{1,0:T(8,128)(2,1)S(1)} %copy-done), custom_call_target="tpu_custom_call" | custom-call | flops 10000000 | bytes 5242880 | tf_op jit(solution)/shard_map/prepare/pallas_call | solution.py:243
  13.8 0.0 copy-start.1
  13.9 1.6 %all-to-all-done.which_ref = s32[32,1,128]{2,1,0:T(1,128)S(1)} async-done(((s32[32,1,128]{2,1,0:T(1,128)}), s32[32,1,128]{2,1,0:T(1,128)S(1)}, u32[]{:S(2)}, u32[]{:S(2)}) %all-to-all-start) | async-done | bytes 16416 | tf_op jit(solution)/shard_map/all_to_all | solution.py:240
  15.5 5.8 %gather.1 = bf16[32,64,128]{2,1,0:T(8,128)(2,1)S(1)} custom-call(s32[32,128]{1,0:T(8,128)S(1)} %bitcast.7, s32[32,1,128]{2,1,0:T(1,128)S(1)} %all-to-all-done.which_ref, f32[4096,1,128]{2,1,0:T(1,128)S(1)} %bitcast.6), custom_call_target="tpu_custom_call" | custom-call | flops 10000000 | bytes 5242880 | tf_op jit(solution)/shard_map/gather/pallas_call | solution.py:258
  21.3 0.0 copy-start.2
  21.3 0.8 %copy-done.2 = bf16[32,64,128]{2,1,0:T(8,128)(2,1)} copy-done((bf16[32,64,128]{2,1,0:T(8,128)(2,1)}, bf16[32,64,128]{2,1,0:T(8,128)(2,1)S(1)}, u32[]{:S(2)}) %copy-start.2) | copy-done | bytes 524312
  22.1 5.8 %all-to-all-start.1 = ((bf16[32,64,128]{2,1,0:T(8,128)(2,1)}), bf16[32,64,128]{2,1,0:T(8,128)(2,1)}, u32[]{:S(2)}, u32[]{:S(2)}) async-start(bf16[32,64,128]{2,1,0:T(8,128)(2,1)} %copy-done.2), calls=%async_computation.1 | async-start | bytes 1048576 | tf_op jit(solution)/shard_map/all_to_all | solution.py:274
  27.9 0.0 copy-done.1
  27.9 0.0 copy-start.7
  28.0 4.6 %local_tiles.1.sum_ref = f32[64,64,128]{2,1,0:T(8,128)S(1)} custom-call(s32[1,640]{1,0:T(1,128)S(1)} %get-tuple-element.13.order_ref, s32[1,768]{1,0:T(1,128)S(1)} %get-tuple-element.14.list_ref, s32[1,128]{1,0:T(1,128)S(1)} %get-tuple-element.15.ends_ref, bf16[64,8192]{1,0:T(8,128)(2,1)S(1)} %copy-done.1, bf16[512,128,128]{2,1,0:T(8,128)(2,1)} %vals_ref.3), custom_call_target="tpu_custom_call" | custom-call | flops 800000000 | bytes 20971520 | tf_op jit(solution)/shard_map/local_tiles/pallas_call | solution.py:281
  32.6 7.0 %all-to-all-done.1.far_ref = bf16[32,64,128]{2,1,0:T(8,128)(2,1)} async-done(((bf16[32,64,128]{2,1,0:T(8,128)(2,1)}), bf16[32,64,128]{2,1,0:T(8,128)(2,1)}, u32[]{:S(2)}, u32[]{:S(2)}) %all-to-all-start.1) | async-done | bytes 524320 | tf_op jit(solution)/shard_map/all_to_all | solution.py:274
  39.6 0.0 copy-done.7
  39.6 0.0 copy-start.3
  39.6 0.0 copy-start.6
  39.6 4.8 %remote_tiles.1 = (bf16[16,64,128]{2,1,0:T(8,128)(2,1)S(1)}, bf16[16,64,128]{2,1,0:T(8,128)(2,1)S(1)}, bf16[16,64,128]{2,1,0:T(8,128)(2,1)S(1)}, bf16[16,64,128]{2,1,0:T(8,128)(2,1)S(1)}) custom-call(s32[1]{0:T(128)} %bitcast.z_ref, s32[1,640]{1,0:T(1,128)S(1)} %get-tuple-element.13.order_ref, s32[1,768]{1,0:T(1,128)S(1)} %get-tuple-element.14.list_ref, ...), custom_call_target="tpu_custom_call" | custom-call | flops 400000000 | bytes 20971520 | tf_op jit(solution)/shard_map/remote_tiles/pallas_call | solution.py:294
  44.3 1.7 %collective-permute-start = (bf16[16,64,128]{2,1,0:T(8,128)(2,1)S(1)}, bf16[16,64,128]{2,1,0:T(8,128)(2,1)S(1)}, u32[]{:S(2)}, u32[]{:S(2)}) collective-permute-start(bf16[16,64,128]{2,1,0:T(8,128)(2,1)S(1)} %get-tuple-element.18), channel_id=1, source_target_pairs={{0,1},{1,2},{2,3},{3,0},{4,5},{5,6},{6,7},{7,4},{8,9},{9,10},{10,1... | collective-permute-start | bytes 786440 | tf_op jit(solution)/shard_map/ppermute | solution.py:312
  46.0 3.3 %collective-permute-start.1 = (bf16[16,64,128]{2,1,0:T(8,128)(2,1)S(1)}, bf16[16,64,128]{2,1,0:T(8,128)(2,1)S(1)}, u32[]{:S(2)}, u32[]{:S(2)}) collective-permute-start(bf16[16,64,128]{2,1,0:T(8,128)(2,1)S(1)} %get-tuple-element.19), channel_id=1, source_target_pairs={{0,2},{1,3},{2,0},{3,1},{4,6},{5,7},{6,4},{7,5},{8,10},{9,11},{10,... | collective-permute-start | bytes 786440 | tf_op jit(solution)/shard_map/ppermute | solution.py:312
  49.4 0.7 %collective-permute-start.2 = (bf16[16,64,128]{2,1,0:T(8,128)(2,1)S(1)}, bf16[16,64,128]{2,1,0:T(8,128)(2,1)S(1)}, u32[]{:S(2)}, u32[]{:S(2)}) collective-permute-start(bf16[16,64,128]{2,1,0:T(8,128)(2,1)S(1)} %get-tuple-element.20), channel_id=1, source_target_pairs={{0,3},{1,0},{2,1},{3,2},{4,7},{5,4},{6,5},{7,6},{8,11},{9,8},{10,9... | collective-permute-start | bytes 786440 | tf_op jit(solution)/shard_map/ppermute | solution.py:312
  50.1 4.0 %collective-permute-done.b_ref = bf16[16,64,128]{2,1,0:T(8,128)(2,1)S(1)} collective-permute-done((bf16[16,64,128]{2,1,0:T(8,128)(2,1)S(1)}, bf16[16,64,128]{2,1,0:T(8,128)(2,1)S(1)}, u32[]{:S(2)}, u32[]{:S(2)}) %collective-permute-start) | collective-permute-done | bytes 262176 | tf_op jit(solution)/shard_map/ppermute | solution.py:312
  54.1 7.1 %collective-permute-done.1.c_ref = bf16[16,64,128]{2,1,0:T(8,128)(2,1)S(1)} collective-permute-done((bf16[16,64,128]{2,1,0:T(8,128)(2,1)S(1)}, bf16[16,64,128]{2,1,0:T(8,128)(2,1)S(1)}, u32[]{:S(2)}, u32[]{:S(2)}) %collective-permute-start.1) | collective-permute-done | bytes 262176 | tf_op jit(solution)/shard_map/ppermute | solution.py:312
  61.2 0.0 collective-permute-done.2.d_ref
  61.2 0.0 copy-done.3
  61.2 0.0 copy-done.6
  61.2 1.5 %project.1 = bf16[2048,256]{1,0:T(8,128)(2,1)} custom-call(s32[1]{0:T(128)} %bitcast.z_ref, bf16[16,64,128]{2,1,0:T(8,128)(2,1)S(1)} %get-tuple-element.17.a_ref, bf16[16,64,128]{2,1,0:T(8,128)(2,1)S(1)} %collective-permute-done.b_ref, bf16[16,64,128]{2,1,0:T(8,128)(2,1)S(1)} %collective-permute-done.1.c_ref, ...), custom_call_target="tpu_custom_call" | custom-call | flops 300000000 | bytes 3145728 | tf_op jit(solution)/shard_map/project/pallas_call | solution.py:318
Async XLA Ops:
  0.0 15.5 %all-to-all-start = ((s32[32,1,128]{2,1,0:T(1,128)}), s32[32,1,128]{2,1,0:T(1,128)S(1)}, u32[]{:S(2)}, u32[]{:S(2)}) async-start(s32[32,1,128]{2,1,0:T(1,128)} %bitcast.10), calls=%async_computation | async-start | bytes 32768 | tf_op jit(solution)/shard_map/all_to_all | solution.py:240
  9.2 1.2 %copy-start = (bf16[64,8192]{1,0:T(8,128)(2,1)S(1)}, bf16[64,8192]{1,0:T(8,128)(2,1)}, u32[]{:S(2)}) copy-start(bf16[64,8192]{1,0:T(8,128)(2,1)} %x_ref.3) | copy-start | bytes 3145732
  10.5 0.7 %copy-start.4 = (s32[1,512]{1,0:T(1,128)S(1)}, s32[1,512]{1,0:T(1,128)}, u32[]{:S(2)}) copy-start(s32[1,512]{1,0:T(1,128)} %row_ref.1) | copy-start | bytes 6148
  11.1 0.7 %copy-start.5 = (s32[1,512]{1,0:T(1,128)S(1)}, s32[1,512]{1,0:T(1,128)}, u32[]{:S(2)}) copy-start(s32[1,512]{1,0:T(1,128)} %col_ref.1) | copy-start | bytes 6148
  13.8 14.1 %copy-start.1 = (bf16[64,8192]{1,0:T(8,128)(2,1)S(1)}, bf16[64,8192]{1,0:T(8,128)(2,1)}, u32[]{:S(2)}) copy-start(bf16[64,8192]{1,0:T(8,128)(2,1)} %x_ref.3) | copy-start | bytes 3145732
  21.3 0.8 %copy-start.2 = (bf16[32,64,128]{2,1,0:T(8,128)(2,1)}, bf16[32,64,128]{2,1,0:T(8,128)(2,1)S(1)}, u32[]{:S(2)}) copy-start(bf16[32,64,128]{2,1,0:T(8,128)(2,1)S(1)} %gather.1) | copy-start | bytes 1572868
  22.1 17.5 %all-to-all-start.1 = ((bf16[32,64,128]{2,1,0:T(8,128)(2,1)}), bf16[32,64,128]{2,1,0:T(8,128)(2,1)}, u32[]{:S(2)}, u32[]{:S(2)}) async-start(bf16[32,64,128]{2,1,0:T(8,128)(2,1)} %copy-done.2), calls=%async_computation.1 | async-start | bytes 1048576 | tf_op jit(solution)/shard_map/all_to_all | solution.py:274
  27.9 11.6 %copy-start.7 = (s32[1,32]{1,0:T(1,128)S(1)}, s32[1,32]{1,0:T(1,128)}, u32[]{:S(2)}) copy-start(s32[1,32]{1,0:T(1,128)} %param.15) | copy-start | bytes 388
  39.6 21.6 %copy-start.3 = (bf16[256,256]{1,0:T(8,128)(2,1)S(1)}, bf16[256,256]{1,0:T(8,128)(2,1)}, u32[]{:S(2)}) copy-start(bf16[256,256]{1,0:T(8,128)(2,1)} %weight_ref.1) | copy-start | bytes 393220
  39.6 21.6 %copy-start.6 = (f32[256]{0:T(256)S(1)}, f32[256]{0:T(256)}, u32[]{:S(2)}) copy-start(f32[256]{0:T(256)} %param.17) | copy-start | bytes 3076
  44.3 9.8 %collective-permute-start = (bf16[16,64,128]{2,1,0:T(8,128)(2,1)S(1)}, bf16[16,64,128]{2,1,0:T(8,128)(2,1)S(1)}, u32[]{:S(2)}, u32[]{:S(2)}) collective-permute-start(bf16[16,64,128]{2,1,0:T(8,128)(2,1)S(1)} %get-tuple-element.18), channel_id=1, source_target_pairs={{0,1},{1,2},{2,3},{3,0},{4,5},{5,6},{6,7},{7,4},{8,9},{9,10},{10,1... | collective-permute-start | bytes 786440 | tf_op jit(solution)/shard_map/ppermute | solution.py:312
  46.0 15.2 %collective-permute-start.1 = (bf16[16,64,128]{2,1,0:T(8,128)(2,1)S(1)}, bf16[16,64,128]{2,1,0:T(8,128)(2,1)S(1)}, u32[]{:S(2)}, u32[]{:S(2)}) collective-permute-start(bf16[16,64,128]{2,1,0:T(8,128)(2,1)S(1)} %get-tuple-element.19), channel_id=1, source_target_pairs={{0,2},{1,3},{2,0},{3,1},{4,6},{5,7},{6,4},{7,5},{8,10},{9,11},{10,... | collective-permute-start | bytes 786440 | tf_op jit(solution)/shard_map/ppermute | solution.py:312
  49.4 11.8 %collective-permute-start.2 = (bf16[16,64,128]{2,1,0:T(8,128)(2,1)S(1)}, bf16[16,64,128]{2,1,0:T(8,128)(2,1)S(1)}, u32[]{:S(2)}, u32[]{:S(2)}) collective-permute-start(bf16[16,64,128]{2,1,0:T(8,128)(2,1)S(1)} %get-tuple-element.20), channel_id=1, source_target_pairs={{0,3},{1,0},{2,1},{3,2},{4,7},{5,4},{6,5},{7,6},{8,11},{9,8},{10,9... | collective-permute-start | bytes 786440 | tf_op jit(solution)/shard_map/ppermute | solution.py:312

commit v3 on v2

--- a/solution.py
+++ b/solution.py
@@ -1,3 +1,5 @@
+import functools
+
 import jax
 import jax.numpy as jnp
 from jax import lax
@@ -5,8 +7,8 @@
 from jax.experimental.pallas import tpu as pltpu
 from jax.sharding import PartitionSpec as P
 
-LOG_U = 4
-U = 1 << LOG_U
+NEAR = 5
+FAR = 4
 LOG_V = 4
 V = 1 << LOG_V
 W = 4
@@ -64,17 +66,28 @@
     (even_c,) = columns(jnp.where(even, 1.0, 0.0))
     rank = count(less) + place
     before = jnp.sum(jnp.where(less, even_c, 0.0), axis=0, keepdims=True)
-    near, far = used & ~is_far, used & is_far
-    near_tiles = total(jnp.where(near, 1.0, 0.0)).astype(I32)
-    used_tiles = total(jnp.where(used, 1.0, 0.0)).astype(I32)
-    near_pairs = total(jnp.where(near & even, 1.0, 0.0)).astype(I32)
-    far_pairs = total(jnp.where(far & even, 1.0, 0.0)).astype(I32)
-    near_groups = (near_pairs + (U - 1)) >> LOG_U
-    far_groups = (far_pairs + (U - 1)) >> LOG_U
-    rank_i = rank.astype(I32)
-    fill = jnp.where(is_far, near_groups * U - near_pairs, 0)
+    part = jnp.where(is_far, 1 + (row >> 4), 0)
+    tiles, groups, first_tile, first_group = [], [], [], []
+    tile_at = pair_at = row[:, :1] * 0
+    filled = row[:, :1] * 0
+    fill = row * 0
+    own = rank.astype(I32)
+    for k in range(5):
+        here = used & (part == k)
+        unit = NEAR if k == 0 else FAR
+        k_tiles = total(jnp.where(here, 1.0, 0.0)).astype(I32)
+        k_pairs = total(jnp.where(here & even, 1.0, 0.0)).astype(I32)
+        k_groups = (k_pairs + ((1 << unit) - 1)) >> unit
+        fill = jnp.where(part == k, filled, fill)
+        own = jnp.where(part == k, own - tile_at, own)
+        first_tile.append(tile_at)
+        first_group.append((pair_at + filled) >> FAR)
+        tiles.append(k_tiles)
+        groups.append(k_groups)
+        tile_at = tile_at + k_tiles
+        pair_at = pair_at + k_pairs
+        filled = filled + (k_groups << unit) - k_pairs
     slot = 2 * (before.astype(I32) + fill) + place.astype(I32)
-    own = rank_i - jnp.where(is_far, near_tiles, 0)
     entry = own | (row << 9) | ((jnp.where(is_far, col - 64, col) + 1) << 15)
     rank_c, slot_c, entry_c = columns(
         jnp.where(used, rank, -1.0),
@@ -88,9 +101,11 @@
     entries = jnp.where(slot_c == s, entry_c, 0.0)
     list_ref[...] = jnp.sum(entries, axis=0, keepdims=True).astype(I32)
     lane = lax.broadcasted_iota(I32, (1, 128), 1)
-    ends = jnp.where(lane == 0, near_tiles, used_tiles)
-    ends = jnp.where(lane == 2, near_groups, ends)
-    ends_ref[...] = jnp.where(lane == 3, far_groups, ends)
+    ends = lane * 0
+    for k in range(5):
+        for i, x in enumerate((first_tile[k], tiles[k], first_group[k], groups[k])):
+            ends = jnp.where(lane == 4 * k + i, x, ends)
+    ends_ref[...] = ends
 
 
 def gather_kernel(idx_ref, which_ref, table_ref, out_ref, even_ref, odd_ref, buf, sem):
@@ -130,39 +145,47 @@
     pltpu.make_async_copy(buf, out_ref, sem).wait()
 
 
-def bring(first, n, order_ref, vals_ref, buf, sems):
+def bring(part, order_ref, ends_ref, vals_ref, buf, sems, base=0):
+    first, n = ends_ref[0, 4 * part], ends_ref[0, 4 * part + 1]
+
     def step(c, _):
         for k in range(V):
             i = c * V + k
             pltpu.make_async_copy(
-                vals_ref.at[order_ref[0, first + i]], buf.at[i], sems.at[c]
+                vals_ref.at[order_ref[0, first + i]], buf.at[base * V + i], sems.at[base + c]
             ).start()
         return 0
 
-    lax.fori_loop(0, (n + (V - 1)) >> LOG_V, step, 0)
-
-
-def add_pairs(first, groups, n, list_ref, block, vals_ref, buf, sems, acc_ref):
     chunks = (n + (V - 1)) >> LOG_V
+    lax.fori_loop(0, chunks, step, 0)
+    return chunks
+
+
+def add_pairs(part, unit, list_ref, ends_ref, block, vals_ref, buf, sems, acc_ref, base=0):
+    n, first, groups = (ends_ref[0, 4 * part + i] for i in (1, 2, 3))
+    chunks = (n + (V - 1)) >> LOG_V
+    size = 1 << unit
+    offset = base * V
 
     def wait(c, _):
-        here = pl.ds(pl.multiple_of(c * V, V), V)
-        pltpu.make_async_copy(vals_ref.at[pl.ds(0, V)], buf.at[here], sems.at[c]).wait()
+        here = pl.ds(pl.multiple_of((base + c) * V, V), V)
+        pltpu.make_async_copy(vals_ref.at[pl.ds(0, V)], buf.at[here], sems.at[base + c]).wait()
         return 0
 
     def step(c, ready):
-        at = 2 * U * (first + c)
-        top = jnp.maximum(list_ref[0, at + 2 * U - 2] & 511, list_ref[0, at + 2 * U - 1] & 511)
+        at = (first << (FAR + 1)) + 2 * size * c
+        top = jnp.maximum(
+            list_ref[0, at + 2 * size - 2] & 511, list_ref[0, at + 2 * size - 1] & 511
+        )
         need = jnp.where(c == groups - 1, chunks, (top >> LOG_V) + 1)
         lax.fori_loop(ready, need, wait, 0)
         found = []
-        for u in range(U):
+        for u in range(size):
             e, f = list_ref[0, at + 2 * u], list_ref[0, at + 2 * u + 1]
             lhs = jnp.concatenate([block(e), block(f)], axis=1)
-            rhs = jnp.concatenate([buf[e & 511], buf[f & 511]], axis=1)
-            found.append(
-                ((e >> 9) & 63, lax.dot_general(lhs, rhs, NT, preferred_element_type=F32))
-            )
+            rhs = jnp.concatenate([buf[offset + (e & 511)], buf[offset + (f & 511)]], axis=1)
+            product = lax.dot_general(lhs, rhs, NT, preferred_element_type=F32)
+            found.append(((e >> 9) & (acc_ref.shape[0] - 1), product))
         for r, product in found:
             acc_ref[r] = acc_ref[r] + product
         return need
@@ -171,8 +194,7 @@
 
 
 def local_kernel(order_ref, list_ref, ends_ref, x_ref, vals_ref, acc_ref, buf, sems):
-    n = ends_ref[0, 0]
-    bring(0, n, order_ref, vals_ref, buf, sems)
+    bring(0, order_ref, ends_ref, vals_ref, buf, sems)
     acc_ref[...] = jnp.zeros_like(acc_ref)
 
     def block(e):
@@ -180,56 +202,68 @@
         x = x_ref[:, pl.ds(pl.multiple_of(c * 128, 128), 128)]
         return jnp.where(e > 0, x, jnp.zeros_like(x))
 
-    add_pairs(0, ends_ref[0, 2], n, list_ref, block, vals_ref, buf, sems, acc_ref)
-
-
-def remote_kernel(
-    z_ref, order_ref, list_ref, ends_ref, count_ref, sum_ref, far_ref, vals_ref, *rest
+    add_pairs(0, NEAR, list_ref, ends_ref, block, vals_ref, buf, sems, acc_ref)
+
+
+def clear(count_ref, far_ref, out_ref):
+    out_ref[0] = jnp.zeros_like(out_ref[0])
+    lane = lax.broadcasted_iota(I32, far_ref.shape[1:], 1)
+
+    def step(q, _):
+        x = far_ref[q]
+        out_ref[q + 1] = jnp.where(lane < count_ref[q], x, jnp.zeros_like(x))
+        return 0
+
+    lax.fori_loop(0, far_ref.shape[0], step, 0, unroll=4)
+
+
+def remote_kernel(shifts, *refs):
+    z_ref, order_ref, list_ref, ends_ref, sum_ref, vals_ref = refs[:6]
+    refs = refs[6:]
+    if shifts[0] == 2:
+        count_ref, raw_ref, out_ref, far_ref, acc_ref, buf, sems = refs
+        out_refs = [out_ref]
+    else:
+        far_ref = refs[0]
+        out_refs = refs[1 : 1 + len(shifts)]
+        acc_ref, buf, sems = refs[1 + len(shifts) :]
+    z = z_ref[0]
+    base, bases = 0, []
+    for k in shifts:
+        bases.append(base)
+        base += bring(1 + ((z + k) & 3), order_ref, ends_ref, vals_ref, buf, sems, base)
+    for i, k in enumerate(shifts):
+        for r in range(16):
+            acc_ref[i, r] = sum_ref[((z + k) & 3) * 16 + r]
+    if shifts[0] == 2:
+        clear(count_ref, raw_ref, far_ref)
+    for i, k in enumerate(shifts):
+        part = 1 + ((z + k) & 3)
+        block = lambda e: far_ref[e >> 15]
+        add_pairs(
+            part, FAR, list_ref, ends_ref, block, vals_ref, buf, sems, acc_ref.at[i], bases[i]
+        )
+        for r in range(16):
+            out_refs[i][r] = acc_ref[i, r].astype(BF)
+
+
+def project_kernel(
+    z_ref, a_ref, b_ref, c_ref, d_ref, weight_ref, bias_ref, out_ref, w_ref, buf, sem
 ):
-    out_refs, (acc_ref, sum_buf, far_buf, sum_sem, buf, sems) = rest[:4], rest[4:]
-    n = ends_ref[0, 1] - ends_ref[0, 0]
-    bring(ends_ref[0, 0], n, order_ref, vals_ref, buf, sems)
-    sum_copy = pltpu.make_async_copy(sum_ref, sum_buf, sum_sem)
-    sum_copy.start()
-    acc_ref[...] = jnp.zeros_like(acc_ref)
-    far_buf[0] = jnp.zeros_like(far_buf[0])
-    lane = lax.broadcasted_iota(I32, far_buf.shape[1:], 1)
-
-    def clear(q, _):
-        x = far_ref[q]
-        far_buf[q + 1] = jnp.where(lane < count_ref[q], x, jnp.zeros_like(x))
-        return 0
-
-    lax.fori_loop(0, far_ref.shape[0], clear, 0, unroll=4)
-    add_pairs(
-        ends_ref[0, 2],
-        ends_ref[0, 3],
-        n,
-        list_ref,
-        lambda e: far_buf[e >> 15],
-        vals_ref,
-        buf,
-        sems,
-        acc_ref,
-    )
-    sum_copy.wait()
-    z = z_ref[0]
-    for k, out_ref in enumerate(out_refs):
-        first = ((z + k) & 3) * 16
-        for r in range(16):
-            out_ref[r] = (acc_ref[first + r] + sum_buf[first + r]).astype(BF)
-
-
-def project_kernel(z_ref, a_ref, b_ref, c_ref, d_ref, weight_ref, bias_ref, out_ref, w_ref):
     z = z_ref[0]
     for k in range(4):
         first = pl.multiple_of(((z - k) & 3) * 64, 64)
         w_ref[64 * k : 64 * k + 64, :] = weight_ref[pl.ds(first, 64), :]
     w = w_ref[...]
-    for r in range(a_ref.shape[0]):
+    n = a_ref.shape[0]
+    for r in range(n):
         x = jnp.concatenate([a_ref[r], b_ref[r], c_ref[r], d_ref[r]], axis=0)
         y = lax.dot_general(x, w, TN, preferred_element_type=F32) + bias_ref[...]
-        out_ref[128 * r : 128 * r + 128, :] = jnp.maximum(y, 0.0).astype(BF)
+        buf[128 * r : 128 * r + 128, :] = jnp.maximum(y, 0.0).astype(BF)
+        if r % 4 == 3:
+            here = pl.ds(128 * (r - 3), 512)
+            pltpu.make_async_copy(buf.at[here], out_ref.at[here], sem).start()
+    pltpu.make_async_copy(buf, out_ref, sem).wait()
 
 
 def on_device(
@@ -245,7 +279,7 @@
         out_shape=(
             jax.ShapeDtypeStruct((v_rows // 2, 128), F32),
             jax.ShapeDtypeStruct((1, n_tiles + 128), I32),
-            jax.ShapeDtypeStruct((1, n_tiles + 128 + 128), I32),
+            jax.ShapeDtypeStruct((1, n_tiles + 384), I32),
             jax.ShapeDtypeStruct((1, 128), I32),
         ),
         in_specs=[SMEM, VMEM, VMEM, VMEM],
@@ -257,7 +291,7 @@
 
     outgoing = pl.pallas_call(
         gather_kernel,
-        out_shape=jax.ShapeDtypeStruct((parts, width, 128), BF),
+        out_shape=pltpu.HBM((parts, width, 128), BF),
         in_specs=[SMEM, VMEM, VMEM],
         out_specs=HBM,
         scratch_shapes=[
@@ -291,36 +325,48 @@
 
     z = lax.axis_index("feat").astype(I32)[None]
     piece = jax.ShapeDtypeStruct((16, width, 128), BF)
-    pieces = pl.pallas_call(
-        remote_kernel,
-        out_shape=(piece,) * 4,
-        in_specs=[SMEM, SMEM, SMEM, SMEM, SMEM, HBM, VMEM, HBM],
-        out_specs=(VMEM,) * 4,
-        scratch_shapes=[
-            pltpu.VMEM(acc.shape, F32),
-            pltpu.VMEM(acc.shape, F32),
-            pltpu.VMEM((parts + 1, width, 128), BF),
-            pltpu.SemaphoreType.DMA,
-        ]
-        + room,
-        compiler_params=params(49),
-        cost_estimate=cost(4 * 10**8, 20 * 2**20),
-        name="remote_tiles",
-    )(z, order, entries, ends, recv_count[0], local, far, tile_vals)
+    far_shape = jax.ShapeDtypeStruct((parts + 1, width, 128), BF)
+
+    def remote(shifts, *more):
+        first = shifts[0] == 2
+        n = len(shifts)
+        rows = n_tiles + V * (n - 1)
+        out = pl.pallas_call(
+            functools.partial(remote_kernel, shifts),
+            out_shape=(piece,) * n + ((far_shape,) if first else ()),
+            in_specs=[SMEM] * 4 + [VMEM, HBM] + ([SMEM, VMEM] if first else [VMEM]),
+            out_specs=(VMEM,) * (n + first),
+            scratch_shapes=[
+                pltpu.VMEM((n, 16, width, 128), F32),
+                pltpu.VMEM((rows, 128, 128), BF),
+                pltpu.SemaphoreType.DMA((rows // V,)),
+            ],
+            compiler_params=params(49),
+            cost_estimate=cost(n * 10**8, 5 * n * 2**20),
+            name="remote_tiles_" + "".join(str(k) for k in shifts),
+        )(z, order, entries, ends, local, tile_vals, *more)
+        return out
 
     def move(x, k):
         return lax.ppermute(x, "feat", [(i, (i + k) % 4) for i in range(4)])
 
-    moved = [pieces[0]] + [None] * 3
-    for k in (2, 1, 3):
-        moved[k] = move(pieces[k], k)
+    moved = [None] * 4
+    out, far = remote((2,), recv_count[0], far)
+    moved[2] = move(out, 2)
+    out = remote((1, 3), far)
+    moved[1], moved[3] = move(out[0], 1), move(out[1], 3)
+    (moved[0],) = remote((0,), far)
 
     return pl.pallas_call(
         project_kernel,
         out_shape=jax.ShapeDtypeStruct((v_rows // 4, weight.shape[1]), BF),
         in_specs=[SMEM] + [VMEM] * 6,
-        out_specs=VMEM,
-        scratch_shapes=[pltpu.VMEM(weight.shape, BF)],
+        out_specs=HBM,
+        scratch_shapes=[
+            pltpu.VMEM(weight.shape, BF),
+            pltpu.VMEM((v_rows // 4, weight.shape[1]), BF),
+            pltpu.SemaphoreType.DMA,
+        ],
         compiler_params=params(6),
         cost_estimate=cost(3 * 10**8, 3 * 2**20),
         name="project",

time: 63.4 us -> 64.1 us (1.011)
  Pallas kernels: 18.7 us -> 22.5 us
  waiting for transfers between devices: 19.7 us -> 17.6 us
  local copies, waits for them, and re-layouts: 3.39 us -> 2.6 us
    pallas_call x2 -> x4, Pallas kernels: 10.6 us -> 14.1 us  [the longest x3 8.35 us: remote(): pl.pallas_call(functools.partial(remote_kernel, shifts), out_shape=(piece...]
    ppermute x3, waiting for transfers between devices: 11.1 us -> 9.54 us  [move(): return lax.ppermute(x, 'feat', [(i, (i + k) % 4) for i in range(4)])]
    unnamed x16 -> x14, local copies, waits for them, and re-layouts: 3.39 us -> 2.6 us
  transfers between devices with their start and end apart: 5 -> 5, of which waited for: 4 -> 5; matrix products, arithmetic and copies ran while one was open for 0% -> 0% of each run, Pallas kernels for 11% -> 15%
where the time goes in v3:
time: 64.1 us; the launch traced here: 63.1 us
  Pallas kernels  22.5 us (35%)
  starting transfers between devices  19.6 us (31%)
  waiting for transfers between devices  17.6 us (27%)
  local copies, waits for them, and re-layouts  2.6 us (4%)
  between operations  0.75 us (1%)
    ppermute x3, waiting for transfers between devices, move(): return lax.ppermute(x, 'feat', [(i, (i + k) % 4) for i in range(4)])  9.54 us
    all_to_all x1, starting transfers between devices, on_device(): lax.all_to_all(recv_rows[0], 'vert', split_axis=0, concat_axis=0, tiled=T...  8.58 us
    pallas_call x3, Pallas kernels, remote(): pl.pallas_call(functools.partial(remote_kernel, shifts), out_shape=(piece...  8.35 us
    all_to_all x1, waiting for transfers between devices, on_device(): lax.all_to_all(outgoing, 'vert', split_axis=0, concat_axis=0, tiled=True)  6.51 us
    all_to_all x1, starting transfers between devices, on_device(): lax.all_to_all(outgoing, 'vert', split_axis=0, concat_axis=0, tiled=True)  5.89 us
    pallas_call x1, Pallas kernels, on_device(): pl.pallas_call(gather_kernel, out_shape=pltpu.HBM((parts, width, 128), BF...  5.72 us
    ppermute x3, starting transfers between devices, move(): return lax.ppermute(x, 'feat', [(i, (i + k) % 4) for i in range(4)])  5.13 us
    pallas_call x1, Pallas kernels, on_device(): pl.pallas_call(local_kernel, out_shape=acc, in_specs=[SMEM, SMEM, SMEM, V...  5.1 us
  transfers between devices with their start and end apart: 5, of which 5 were waited for; matrix products, arithmetic and copies ran while one was open for 0% of the time, Pallas kernels for 15%

profile of v3, /device:TPU:1, one launch (start us, length us, event | category | flops | bytes accessed | tf_op | source)
XLA Modules:
  0.0 63.1 jit_solution(10399737174344058573)
XLA Ops:
  0.0 8.6 %all-to-all-start = ((s32[32,1,128]{2,1,0:T(1,128)}), s32[32,1,128]{2,1,0:T(1,128)S(1)}, u32[]{:S(2)}, u32[]{:S(2)}) async-start(s32[32,1,128]{2,1,0:T(1,128)} %bitcast.10), calls=%async_computation | async-start | bytes 32768 | tf_op jit(solution)/shard_map/all_to_all | solution.py:274
  9.2 0.0 copy-start
  9.2 1.2 %copy-done = bf16[64,8192]{1,0:T(8,128)(2,1)S(1)} copy-done((bf16[64,8192]{1,0:T(8,128)(2,1)S(1)}, bf16[64,8192]{1,0:T(8,128)(2,1)}, u32[]{:S(2)}) %copy-start) | copy-done | bytes 1048600
  10.5 0.0 copy-start.3
  10.5 0.7 %copy-done.3 = s32[1,512]{1,0:T(1,128)S(1)} copy-done((s32[1,512]{1,0:T(1,128)S(1)}, s32[1,512]{1,0:T(1,128)}, u32[]{:S(2)}) %copy-start.3) | copy-done | bytes 2072
  11.1 0.0 copy-start.4
  11.1 0.7 %copy-done.4 = s32[1,512]{1,0:T(1,128)S(1)} copy-done((s32[1,512]{1,0:T(1,128)S(1)}, s32[1,512]{1,0:T(1,128)}, u32[]{:S(2)}) %copy-start.4) | copy-done | bytes 2072
  11.8 2.1 %prepare.1 = (f32[4096,128]{1,0:T(8,128)S(1)}, s32[1,640]{1,0:T(1,128)S(1)}, s32[1,896]{1,0:T(1,128)S(1)}, s32[1,128]{1,0:T(1,128)S(1)}) custom-call(s32[1]{0:T(128)S(6)} %copy.10.count_ref, s32[1,512]{1,0:T(1,128)S(1)} %copy-done.3, s32[1,512]{1,0:T(1,128)S(1)} %copy-done.4, bf16[64,8192]{1,0:T(8,128)(2,1)S(1)} %copy-done), custom_call_target="tpu_custom_call" | custom-call | flops 10000000 | bytes 5242880 | tf_op jit(solution)/shard_map/prepare/pallas_call | solution.py:277
  13.9 0.0 copy-start.1
  13.9 1.6 %all-to-all-done.which_ref = s32[32,1,128]{2,1,0:T(1,128)S(1)} async-done(((s32[32,1,128]{2,1,0:T(1,128)}), s32[32,1,128]{2,1,0:T(1,128)S(1)}, u32[]{:S(2)}, u32[]{:S(2)}) %all-to-all-start) | async-done | bytes 16416 | tf_op jit(solution)/shard_map/all_to_all | solution.py:274
  15.5 5.7 %gather.1 = bf16[32,64,128]{2,1,0:T(8,128)(2,1)} custom-call(s32[32,128]{1,0:T(8,128)S(1)} %bitcast.7, s32[32,1,128]{2,1,0:T(1,128)S(1)} %all-to-all-done.which_ref, f32[4096,1,128]{2,1,0:T(1,128)S(1)} %bitcast.6), custom_call_target="tpu_custom_call" | custom-call | flops 10000000 | bytes 5242880 | tf_op jit(solution)/shard_map/gather/pallas_call | solution.py:292
  21.2 5.9 %all-to-all-start.1 = ((bf16[32,64,128]{2,1,0:T(8,128)(2,1)}), bf16[32,64,128]{2,1,0:T(8,128)(2,1)}, u32[]{:S(2)}, u32[]{:S(2)}) async-start(bf16[32,64,128]{2,1,0:T(8,128)(2,1)} %gather.1), calls=%async_computation.1 | async-start | bytes 1048576 | tf_op jit(solution)/shard_map/all_to_all | solution.py:308
  27.1 0.0 copy-done.1
  27.1 0.0 copy-start.6
  27.1 5.1 %local_tiles.1.refs_4_ = f32[64,64,128]{2,1,0:T(8,128)S(1)} custom-call(s32[1,640]{1,0:T(1,128)S(1)} %get-tuple-element.13.order_ref.refs_1_, s32[1,896]{1,0:T(1,128)S(1)} %get-tuple-element.14.list_ref.refs_2_, s32[1,128]{1,0:T(1,128)S(1)} %get-tuple-element.15.ends_ref.refs_3_, bf16[64,8192]{1,0:T(8,128)(2,1)S(1)} %copy-done.1, bf16[512,128,128]{2,1,0:T(8,128)(2,1)} %refs_5_.5), custom_call_target="tpu_custom_call" | custom-call | flops 800000000 | bytes 20971520 | tf_op jit(solution)/shard_map/local_tiles/pallas_call | solution.py:315
  32.3 6.5 %all-to-all-done.1.refs_7_ = bf16[32,64,128]{2,1,0:T(8,128)(2,1)} async-done(((bf16[32,64,128]{2,1,0:T(8,128)(2,1)}), bf16[32,64,128]{2,1,0:T(8,128)(2,1)}, u32[]{:S(2)}, u32[]{:S(2)}) %all-to-all-start.1) | async-done | bytes 524320 | tf_op jit(solution)/shard_map/all_to_all | solution.py:308
  38.8 0.0 copy-done.6
  38.8 2.9 %remote_tiles_2.1 = (bf16[16,64,128]{2,1,0:T(8,128)(2,1)S(1)}, bf16[33,64,128]{2,1,0:T(8,128)(2,1)S(1)}) custom-call(s32[1]{0:T(128)} %bitcast.refs_0_.z_ref, s32[1,640]{1,0:T(1,128)S(1)} %get-tuple-element.13.order_ref.refs_1_, s32[1,896]{1,0:T(1,128)S(1)} %get-tuple-element.14.list_ref.refs_2_, s32[1,128]{1,0:T(1,128)S(1)} %get-tuple-element.15.ends_ref.refs_3_, ...), custom_call_target="tpu_custom_call" | custom-call | flops 100000000 | bytes 5242880 | tf_op jit(solution)/shard_map/remote_tiles_2/pallas_call | solution.py:334
  41.6 3.0 %remote_tiles_13.1 = (bf16[16,64,128]{2,1,0:T(8,128)(2,1)S(1)}, bf16[16,64,128]{2,1,0:T(8,128)(2,1)S(1)}) custom-call(s32[1]{0:T(128)} %bitcast.refs_0_.z_ref, s32[1,640]{1,0:T(1,128)S(1)} %get-tuple-element.13.order_ref.refs_1_, s32[1,896]{1,0:T(1,128)S(1)} %get-tuple-element.14.list_ref.refs_2_, s32[1,128]{1,0:T(1,128)S(1)} %get-tuple-element.15.ends_ref.refs_3_, ...), custom_call_target="tpu_custom_call" | custom-call | flops 200000000 | bytes 10485760 | tf_op jit(solution)/shard_map/remote_tiles_13/pallas_call | solution.py:334
  44.7 1.7 %collective-permute-start = (bf16[16,64,128]{2,1,0:T(8,128)(2,1)S(1)}, bf16[16,64,128]{2,1,0:T(8,128)(2,1)S(1)}, u32[]{:S(2)}, u32[]{:S(2)}) collective-permute-start(bf16[16,64,128]{2,1,0:T(8,128)(2,1)S(1)} %get-tuple-element.18), channel_id=1, source_target_pairs={{0,1},{1,2},{2,3},{3,0},{4,5},{5,6},{6,7},{7,4},{8,9},{9,10},{10,1... | collective-permute-start | bytes 786440 | tf_op jit(solution)/shard_map/ppermute | solution.py:351
  46.4 2.2 %collective-permute-start.2 = (bf16[16,64,128]{2,1,0:T(8,128)(2,1)S(1)}, bf16[16,64,128]{2,1,0:T(8,128)(2,1)S(1)}, u32[]{:S(2)}, u32[]{:S(2)}) collective-permute-start(bf16[16,64,128]{2,1,0:T(8,128)(2,1)S(1)} %get-tuple-element.20), channel_id=1, source_target_pairs={{0,3},{1,0},{2,1},{3,2},{4,7},{5,4},{6,5},{7,6},{8,11},{9,8},{10,9... | collective-permute-start | bytes 786440 | tf_op jit(solution)/shard_map/ppermute | solution.py:351
  48.6 0.0 copy-start.2
  48.6 0.0 copy-start.5
  48.6 1.2 %collective-permute-start.1 = (bf16[16,64,128]{2,1,0:T(8,128)(2,1)S(1)}, bf16[16,64,128]{2,1,0:T(8,128)(2,1)S(1)}, u32[]{:S(2)}, u32[]{:S(2)}) collective-permute-start(bf16[16,64,128]{2,1,0:T(8,128)(2,1)S(1)} %get-tuple-element.19), channel_id=1, source_target_pairs={{0,2},{1,3},{2,0},{3,1},{4,6},{5,7},{6,4},{7,5},{8,10},{9,11},{10,... | collective-permute-start | bytes 786440 | tf_op jit(solution)/shard_map/ppermute | solution.py:351
  49.8 2.5 %remote_tiles_0.1.a_ref = bf16[16,64,128]{2,1,0:T(8,128)(2,1)S(1)} custom-call(s32[1]{0:T(128)} %bitcast.refs_0_.z_ref, s32[1,640]{1,0:T(1,128)S(1)} %get-tuple-element.13.order_ref.refs_1_, s32[1,896]{1,0:T(1,128)S(1)} %get-tuple-element.14.list_ref.refs_2_, s32[1,128]{1,0:T(1,128)S(1)} %get-tuple-element.15.ends_ref.refs_3_, ...), custom_call_target="tpu_custom_call" | custom-call | flops 100000000 | bytes 5242880 | tf_op jit(solution)/shard_map/remote_tiles_0/pallas_call | solution.py:334
  52.3 3.0 %collective-permute-done.b_ref = bf16[16,64,128]{2,1,0:T(8,128)(2,1)S(1)} collective-permute-done((bf16[16,64,128]{2,1,0:T(8,128)(2,1)S(1)}, bf16[16,64,128]{2,1,0:T(8,128)(2,1)S(1)}, u32[]{:S(2)}, u32[]{:S(2)}) %collective-permute-start) | collective-permute-done | bytes 262176 | tf_op jit(solution)/shard_map/ppermute | solution.py:351
  55.3 4.5 %collective-permute-done.2.d_ref = bf16[16,64,128]{2,1,0:T(8,128)(2,1)S(1)} collective-permute-done((bf16[16,64,128]{2,1,0:T(8,128)(2,1)S(1)}, bf16[16,64,128]{2,1,0:T(8,128)(2,1)S(1)}, u32[]{:S(2)}, u32[]{:S(2)}) %collective-permute-start.2) | collective-permute-done | bytes 262176 | tf_op jit(solution)/shard_map/ppermute | solution.py:351
  59.8 2.0 %collective-permute-done.1.c_ref = bf16[16,64,128]{2,1,0:T(8,128)(2,1)S(1)} collective-permute-done((bf16[16,64,128]{2,1,0:T(8,128)(2,1)S(1)}, bf16[16,64,128]{2,1,0:T(8,128)(2,1)S(1)}, u32[]{:S(2)}, u32[]{:S(2)}) %collective-permute-start.1) | collective-permute-done | bytes 262176 | tf_op jit(solution)/shard_map/ppermute | solution.py:351
  61.8 0.0 copy-done.2
  61.8 0.0 copy-done.5
  61.8 1.3 %project.1 = bf16[2048,256]{1,0:T(8,128)(2,1)} custom-call(s32[1]{0:T(128)} %bitcast.refs_0_.z_ref, bf16[16,64,128]{2,1,0:T(8,128)(2,1)S(1)} %remote_tiles_0.1.a_ref, bf16[16,64,128]{2,1,0:T(8,128)(2,1)S(1)} %collective-permute-done.b_ref, bf16[16,64,128]{2,1,0:T(8,128)(2,1)S(1)} %collective-permute-done.1.c_ref, ...), custom_call_target="tpu_custom_call" | custom-call | flops 300000000 | bytes 3145728 | tf_op jit(solution)/shard_map/project/pallas_call | solution.py:360
Async XLA Ops:
  0.0 15.5 %all-to-all-start = ((s32[32,1,128]{2,1,0:T(1,128)}), s32[32,1,128]{2,1,0:T(1,128)S(1)}, u32[]{:S(2)}, u32[]{:S(2)}) async-start(s32[32,1,128]{2,1,0:T(1,128)} %bitcast.10), calls=%async_computation | async-start | bytes 32768 | tf_op jit(solution)/shard_map/all_to_all | solution.py:274
  9.2 1.2 %copy-start = (bf16[64,8192]{1,0:T(8,128)(2,1)S(1)}, bf16[64,8192]{1,0:T(8,128)(2,1)}, u32[]{:S(2)}) copy-start(bf16[64,8192]{1,0:T(8,128)(2,1)} %x_ref.3) | copy-start | bytes 3145732
  10.5 0.7 %copy-start.3 = (s32[1,512]{1,0:T(1,128)S(1)}, s32[1,512]{1,0:T(1,128)}, u32[]{:S(2)}) copy-start(s32[1,512]{1,0:T(1,128)} %row_ref.1) | copy-start | bytes 6148
  11.1 0.7 %copy-start.4 = (s32[1,512]{1,0:T(1,128)S(1)}, s32[1,512]{1,0:T(1,128)}, u32[]{:S(2)}) copy-start(s32[1,512]{1,0:T(1,128)} %col_ref.1) | copy-start | bytes 6148
  13.9 13.2 %copy-start.1 = (bf16[64,8192]{1,0:T(8,128)(2,1)S(1)}, bf16[64,8192]{1,0:T(8,128)(2,1)}, u32[]{:S(2)}) copy-start(bf16[64,8192]{1,0:T(8,128)(2,1)} %x_ref.3) | copy-start | bytes 3145732
  21.2 17.5 %all-to-all-start.1 = ((bf16[32,64,128]{2,1,0:T(8,128)(2,1)}), bf16[32,64,128]{2,1,0:T(8,128)(2,1)}, u32[]{:S(2)}, u32[]{:S(2)}) async-start(bf16[32,64,128]{2,1,0:T(8,128)(2,1)} %gather.1), calls=%async_computation.1 | async-start | bytes 1048576 | tf_op jit(solution)/shard_map/all_to_all | solution.py:308
  27.1 11.6 %copy-start.6 = (s32[1,32]{1,0:T(1,128)S(1)}, s32[1,32]{1,0:T(1,128)}, u32[]{:S(2)}) copy-start(s32[1,32]{1,0:T(1,128)} %param.15) | copy-start | bytes 388
  44.7 10.6 %collective-permute-start = (bf16[16,64,128]{2,1,0:T(8,128)(2,1)S(1)}, bf16[16,64,128]{2,1,0:T(8,128)(2,1)S(1)}, u32[]{:S(2)}, u32[]{:S(2)}) collective-permute-start(bf16[16,64,128]{2,1,0:T(8,128)(2,1)S(1)} %get-tuple-element.18), channel_id=1, source_target_pairs={{0,1},{1,2},{2,3},{3,0},{4,5},{5,6},{6,7},{7,4},{8,9},{9,10},{10,1... | collective-permute-start | bytes 786440 | tf_op jit(solution)/shard_map/ppermute | solution.py:351
  46.4 13.4 %collective-permute-start.2 = (bf16[16,64,128]{2,1,0:T(8,128)(2,1)S(1)}, bf16[16,64,128]{2,1,0:T(8,128)(2,1)S(1)}, u32[]{:S(2)}, u32[]{:S(2)}) collective-permute-start(bf16[16,64,128]{2,1,0:T(8,128)(2,1)S(1)} %get-tuple-element.20), channel_id=1, source_target_pairs={{0,3},{1,0},{2,1},{3,2},{4,7},{5,4},{6,5},{7,6},{8,11},{9,8},{10,9... | collective-permute-start | bytes 786440 | tf_op jit(solution)/shard_map/ppermute | solution.py:351
  48.6 13.2 %copy-start.2 = (bf16[256,256]{1,0:T(8,128)(2,1)S(1)}, bf16[256,256]{1,0:T(8,128)(2,1)}, u32[]{:S(2)}) copy-start(bf16[256,256]{1,0:T(8,128)(2,1)} %weight_ref.1) | copy-start | bytes 393220
  48.6 13.2 %copy-start.5 = (f32[256]{0:T(256)S(1)}, f32[256]{0:T(256)}, u32[]{:S(2)}) copy-start(f32[256]{0:T(256)} %param.17) | copy-start | bytes 3076
  48.6 13.2 %collective-permute-start.1 = (bf16[16,64,128]{2,1,0:T(8,128)(2,1)S(1)}, bf16[16,64,128]{2,1,0:T(8,128)(2,1)S(1)}, u32[]{:S(2)}, u32[]{:S(2)}) collective-permute-start(bf16[16,64,128]{2,1,0:T(8,128)(2,1)S(1)} %get-tuple-element.19), channel_id=1, source_target_pairs={{0,2},{1,3},{2,0},{3,1},{4,6},{5,7},{6,4},{7,5},{8,10},{9,11},{10,... | collective-permute-start | bytes 786440 | tf_op jit(solution)/shard_map/ppermute | solution.py:351
